TPU v7x, 256 devices: a whole 4x4x8 slice. The times are simulated.
256 devices in a mesh: prow: 32 (over z, x), pcol: 8 (over y, core).
Axes of the slice: x: 4, y: 4, z: 8, core: 2. Of those that a mesh axis runs over, the one named last changes fastest.
Arguments:
- cross_cov: float32 [1, 32, 256, 4, 8, 256], P(None, 'prow', None, None, 'pcol'), may hold values from -6 to 6
- left_factor: float32 [1, 32, 256, 512], P(None, 'prow', None, 'pcol'), may hold values from -1 to 3, as said below
- right_factor: float32 [4, 8, 256, 512], P(None, 'pcol', None, 'prow'), may hold values from -1 to 3, as said below
Outputs:
- whitened: float32 [1, 32, 256, 4, 8, 256], P(None, 'prow', None, None, 'pcol')
Inputs may be any that keep to these rules, and one draw needn't show every extreme that they name: `left_factor`: the diagonal entries of the diagonal blocks lie between 1.5 and 2. `right_factor`: the diagonal entries of the diagonal blocks lie between 1.5 and 2.
All inputs are finite; a program needn't handle non-finite values.
Results may differ from a plain program's by a relative error of at most 0.0001.
Values sent between devices are 32-bit elements; how exact they have to be, the bound alone decides.
A program may use at most 64 MiB of HBM per device.

v0:
```python
import jax
import jax.numpy as jnp
from jax import lax
from jax.sharding import Mesh
from jax.sharding import PartitionSpec as P

STEPS = 2
PROW = ("prow_0", "prow_1")


def sent_to_all(x, axis):
    length = lax.axis_size(axis)
    return lax.all_to_all(jnp.broadcast_to(x[None], (length, *x.shape)), axis, 0, 0, tiled=True)


def in_order(pieces, dim):
    shape = list(pieces.shape[1:])
    shape[dim] *= pieces.shape[0]
    return jnp.moveaxis(pieces, 0, dim).reshape(shape)


def gather_directly(x, axis, dim):
    pieces = sent_to_all(x, axis)
    return in_order(pieces, dim)


def gathered_by_axis(x, axes, dim):
    if not axes:
        return x
    nearer = lax.all_gather(x, axes[-1], axis=dim, tiled=True)
    return gathered_by_axis(nearer, axes[:-1], dim)


def broadcast_by_axis(x, axes, root):
    x = jnp.where(lax.axis_index(axes) == root, x, jnp.zeros_like(x))
    for axis in axes:
        x = lax.psum(x, axis)
    return x


def picked(x, axis, root):
    return lax.dynamic_index_in_dim(lax.all_gather(x, axis), root, 0, keepdims=False)


def solve_left(operands):
    diag_block, owned_rows = operands
    return jax.scipy.linalg.solve_triangular(diag_block, owned_rows, lower=True)


def solve_right(operands):
    diag_block, owned_cols = operands
    return jax.scipy.linalg.solve_triangular(diag_block, owned_cols.T, lower=True).T


def shards(cross_cov, left_factor, right_factor):
    rows_axis = lax.axis_size(PROW)
    cols_axis = lax.axis_size("pcol")
    my_row = lax.axis_index(PROW)
    my_col = lax.axis_index("pcol")
    row_blocks = cross_cov.shape[0]
    block_size = cross_cov.shape[2]
    col_blocks = cross_cov.shape[3]
    left_rows = gather_directly(left_factor, "pcol", 3)[:, 0]
    right_rows = gathered_by_axis(right_factor, PROW, 3)[:, 0]
    matrix = cross_cov.reshape(row_blocks, block_size, col_blocks * block_size)
    row_index = (jnp.arange(row_blocks) * rows_axis + my_row).reshape(row_blocks, 1, 1)

    def left_update(current, solved, block_step):
        first_col = block_step * block_size
        factor = left_rows[:, :, first_col : first_col + block_size]
        update = jnp.einsum("cij,jn->cin", factor, solved, precision=lax.Precision.HIGHEST)
        return jnp.where(
            row_index > block_step,
            current - update,
            jnp.where(row_index == block_step, solved[None], current),
        )

    received = []
    for block_step in range(STEPS):
        local_block = block_step // rows_axis
        received.append(
            (
                broadcast_by_axis(matrix[local_block], PROW, block_step % rows_axis),
                broadcast_by_axis(left_rows[local_block], PROW, block_step % rows_axis),
            )
        )
    solved_list = []
    for block_step in range(STEPS):
        unsolved, panel_rows = received[block_step]
        for earlier in range(block_step):
            factor = panel_rows[:, earlier * block_size : (earlier + 1) * block_size]
            unsolved = unsolved - jnp.dot(
                factor, solved_list[earlier], precision=lax.Precision.HIGHEST
            )
        diag_block = panel_rows[:, block_step * block_size : (block_step + 1) * block_size]
        solved_list.append(solve_left((diag_block, unsolved)))
    for block_step in range(STEPS):
        matrix = left_update(matrix, solved_list[block_step], block_step)
    columns = matrix.reshape(row_blocks * block_size, col_blocks, block_size)
    col_index = (jnp.arange(col_blocks) * cols_axis + my_col).reshape(1, col_blocks, 1)

    def right_update(current, solved, block_step):
        first_col = block_step * block_size
        factor = right_rows[:, :, first_col : first_col + block_size]
        update = jnp.einsum("rj,dsj->rds", solved, factor, precision=lax.Precision.HIGHEST)
        return jnp.where(
            col_index > block_step,
            current - update,
            jnp.where(col_index == block_step, solved[:, None, :], current),
        )

    received = []
    for block_step in range(STEPS):
        local_block = block_step // cols_axis
        received.append(
            (
                picked(columns[:, local_block], "pcol", block_step % cols_axis),
                picked(right_rows[local_block], "pcol", block_step % cols_axis),
            )
        )
    solved_list = []
    for block_step in range(STEPS):
        unsolved, panel_rows = received[block_step]
        for earlier in range(block_step):
            factor = panel_rows[:, earlier * block_size : (earlier + 1) * block_size]
            unsolved = unsolved - jnp.dot(
                solved_list[earlier], factor.T, precision=lax.Precision.HIGHEST
            )
        diag_block = panel_rows[:, block_step * block_size : (block_step + 1) * block_size]
        solved_list.append(solve_right((diag_block, unsolved)))
    for block_step in range(STEPS):
        columns = right_update(columns, solved_list[block_step], block_step)
    return columns.reshape(cross_cov.shape)


def solution(mesh):
    torus = Mesh(mesh.devices.reshape(8, 4, mesh.shape["pcol"]), ("prow_0", "prow_1", "pcol"))
    return jax.shard_map(
        shards,
        mesh=torus,
        in_specs=(
            P(None, PROW, None, None, "pcol", None),
            P(None, PROW, None, "pcol"),
            P(None, "pcol", None, PROW),
        ),
        out_specs=P(None, PROW, None, None, "pcol", None),
        check_vma=False,
    )
```

profile of v0, /device:TPU:151, one launch (start us, length us, event | category | flops | bytes accessed | tf_op | source)
XLA Modules:
  0.0 403.2 jit_solution(18186015079904050890)
XLA Ops:
  6.5 1.8 broadcast_in_dim.75
  8.3 5.1 %all-to-all-start = ((f32[8,1,1,256,64]{3,4,2,1,0:T(8,128)}), f32[8,1,1,256,64]{3,4,2,1,0:T(8,128)S(1)}, u32[]{:S(2)}, u32[]{:S(2)}) async-start(f32[8,1,1,256,64]{3,4,2,1,0:T(8,128)} %broadcast_in_dim.75), calls=%async_computation | async-start | bytes 1048576 | tf_op jit(solution)/shard_map/all_to_all | solution.py:13
  13.4 3.0 reduce
  16.6 1.6 broadcast_select_fusion
  18.1 2.2 all-to-all-done
  20.4 1.1 bitcast_select_fusion.1
  21.6 91.1 %all-reduce.5.cloned.1.call-done = (f32[256,1024]{1,0:T(8,128)}, f32[256,512]{0,1:T(8,128)}, f32[256,1024]{1,0:T(8,128)}, f32[256,512]{0,1:T(8,128)}) async-done(((f32[256,1024]{1,0:T(8,128)}, f32[256,512]{0,1:T(8,128)}, f32[256,1024]{1,0:T(8,128)}, f32[256,512]{0,1:T(8,128)}), (f32[256,1024]{1,0:T(8,128)}, f32[256,512]{0,1:T(8,128)}, f32[256,1024]{1,0:T(8,128)}, ...) | async-done | bytes 3145744 | tf_op jit(solution)/shard_map/psum | solution.py:37
  112.8 10.1 %all_gather.14 = f32[4,1,256,64]{2,0,1,3:T(4,128)} all-gather(f32[4,1,256,16]{2,0,1,3:T(4,128)S(1)} %copy.34), channel_id=1, replica_groups=mesh['prow_0'=8,'prow_1'=4,'pcol'=8] {'prow_1'}, dimensions={3}, use_global_device_ids=true | all-gather | bytes 327680 | tf_op jit(solution)/shard_map/all_gather | solution.py:30
  123.0 72.4 %all-reduce.7.cloned.1.call-done = (f32[256,1024]{1,0:T(8,128)}, f32[256,512]{0,1:T(8,128)}, f32[256,1024]{1,0:T(8,128)}, f32[256,512]{0,1:T(8,128)}) async-done(((f32[256,1024]{1,0:T(8,128)}, f32[256,512]{0,1:T(8,128)}, f32[256,1024]{1,0:T(8,128)}, f32[256,512]{0,1:T(8,128)}), (f32[256,1024]{1,0:T(8,128)}, f32[256,512]{0,1:T(8,128)}, f32[256,1024]{1,0:T(8,128)}, ...) | async-done | bytes 3145744 | tf_op jit(solution)/shard_map/psum | solution.py:37
  195.4 1.1 slice_select_fusion.2
  196.6 4.3 %while.8 = (s32[]{:T(128)}, f32[256,256]{0,1:T(8,128)S(1)}, s32[2,2]{1,0:T(2,128)S(1)}, f32[2,128,128]{2,1,0:T(8,128)S(1)}, s32[]{:T(128)}) while((s32[]{:T(128)}, f32[256,256]{0,1:T(8,128)S(1)}, s32[2,2]{1,0:T(2,128)S(1)}, f32[2,128,128]{2,1,0:T(8,128)S(1)}, s32[]{:T(128)}) %tuple.76), condition=%wide.while_cond, body=%wide.while_body.sunk | while | flops 2 | bytes 393321 | solution.py:47
  197.2 1.4 dynamic-slice.25
  199.3 1.4 dynamic-slice.25
  200.8 19.7 %custom-call.8 = f32[2,128,128]{1,2,0:T(8,128)S(1)} custom-call(f32[2,128,128]{2,1,0:T(8,128)S(1)} %get-tuple-element.35), custom_call_target="InvertDiagBlocksLowerTriangular" | custom-call | tf_op jit(solution)/shard_map/jit(_solve_triangular)/triangular_solve | solution.py:47
  220.5 4.2 %while.9 = (s32[]{:T(128)}, f32[256,256]{0,1:T(8,128)S(1)}, s32[2,2]{1,0:T(2,128)S(1)}, f32[2,128,128]{2,1,0:T(8,128)S(1)}, s32[]{:T(128)}) while((s32[]{:T(128)}, f32[256,256]{0,1:T(8,128)S(1)}, s32[2,2]{1,0:T(2,128)S(1)}, f32[2,128,128]{2,1,0:T(8,128)S(1)}, s32[]{:T(128)}) %tuple.100), condition=%wide.while_cond.clone, body=%wide.while_body.clone.sunk | while | flops 2 | bytes 393321 | solution.py:47
  221.2 1.3 dynamic-slice.27
  223.2 1.3 dynamic-slice.27
  224.7 19.9 %custom-call.9 = f32[2,128,128]{1,2,0:T(8,128)S(1)} custom-call(f32[2,128,128]{2,1,0:T(8,128)S(1)} %get-tuple-element.36), custom_call_target="InvertDiagBlocksLowerTriangular" | custom-call | tf_op jit(solution)/shard_map/jit(_solve_triangular)/triangular_solve | solution.py:47
  246.6 1.1 convolution_subtract_fusion.2
  249.6 1.3 fusion.1
  250.8 1.2 fusion.3
  253.7 2.0 slice.113
  255.7 1.6 copy.35
  257.3 1.9 copy.37
  259.3 23.7 %all-gather.10.cloned.1.call-done = f32[2048,1,256]{0,2,1:T(8,128)} async-done(((f32[256,1,256]{0,2,1:T(8,128)}), f32[2048,1,256]{0,2,1:T(8,128)}) %all-gather.10.cloned.1.call-update) | async-done | bytes 2097168 | tf_op jit(solution)/shard_map/all_gather | solution.py:42
  283.0 1.7 slice_bitcast_fusion.3
  284.7 34.7 %all-gather.8.cloned.1.call-done = f32[8,1,256,512]{3,2,1,0:T(8,128)} async-done(((f32[1,1,256,512]{3,2,1,0:T(8,128)}), f32[8,1,256,512]{3,2,1,0:T(8,128)}) %all-gather.8.cloned.1.call-update) | async-done | bytes 4194320 | tf_op jit(solution)/shard_map/all_gather | solution.py:42
  319.3 2.1 slice_bitcast_fusion
  321.4 1.7 slice_select_fusion
  323.1 5.4 %while.10 = (s32[]{:T(128)}, f32[256,256]{1,0:T(8,128)S(1)}, s32[2,2]{1,0:T(2,128)}, f32[2,128,128]{2,1,0:T(8,128)S(1)}, s32[]{:T(128)}) while((s32[]{:T(128)}, f32[256,256]{1,0:T(8,128)S(1)}, s32[2,2]{1,0:T(2,128)}, f32[2,128,128]{2,1,0:T(8,128)S(1)}, s32[]{:T(128)}) %tuple.101), condition=%wide.while_cond.1, body=%wide.while_body.1.sunk | while | flops 2 | bytes 131181 | solution.py:52
  324.4 1.4 bitcast_dynamic-update-slice_fusion.10
  327.1 1.4 bitcast_dynamic-update-slice_fusion.10
  328.5 20.3 %custom-call.10 = f32[2,128,128]{1,2,0:T(8,128)} custom-call(f32[2,128,128]{2,1,0:T(8,128)S(1)} %get-tuple-element.37), custom_call_target="InvertDiagBlocksLowerTriangular" | custom-call | tf_op jit(solution)/shard_map/jit(_solve_triangular)/triangular_solve | solution.py:52
  348.8 1.2 fusion.22
  350.1 1.2 convolution_subtract_fusion.7
  351.2 1.1 fusion.27
  352.4 7.2 %while.11 = (s32[]{:T(128)}, f32[256,256]{1,0:T(8,128)}, s32[2,2]{1,0:T(2,128)}, f32[2,128,128]{2,1,0:T(8,128)S(1)}, s32[]{:T(128)}) while((s32[]{:T(128)}, f32[256,256]{1,0:T(8,128)}, s32[2,2]{1,0:T(2,128)}, f32[2,128,128]{2,1,0:T(8,128)S(1)}, s32[]{:T(128)}) %tuple.102), condition=%wide.while_cond.1.clone, body=%wide.while_body.1.clone.sunk | while | flops 2 | bytes 131181 | solution.py:52
  353.7 2.3 bitcast_dynamic-update-slice_fusion.11
  357.4 2.3 bitcast_dynamic-update-slice_fusion.11
  359.6 20.3 %custom-call.11 = f32[2,128,128]{1,2,0:T(8,128)} custom-call(f32[2,128,128]{2,1,0:T(8,128)S(1)} %get-tuple-element.38), custom_call_target="InvertDiagBlocksLowerTriangular" | custom-call | tf_op jit(solution)/shard_map/jit(_solve_triangular)/triangular_solve | solution.py:52
  380.6 1.4 fusion.7
  382.1 1.1 fusion.20
  383.2 1.1 convolution_subtract_fusion.6
  386.0 1.8 copy.44
  387.8 1.8 copy.40
  389.6 3.0 fusion.6
  392.6 2.0 fusion.5
  394.6 2.1 copy.45
  (77 shorter events, 16.4 us)
Async XLA Ops:
  6.5 6.8 %copy-start.2 = (f32[1,1,256,4,1,256]{5,4,3,2,1,0:T(1,128)S(1)}, f32[1,1,256,4,1,256]{5,4,3,2,1,0:T(1,128)}, u32[]{:S(2)}) copy-start(f32[1,1,256,4,1,256]{5,4,3,2,1,0:T(1,128)} %param.7) | copy-start | bytes 3145732
  8.3 12.1 %all-to-all-start = ((f32[8,1,1,256,64]{3,4,2,1,0:T(8,128)}), f32[8,1,1,256,64]{3,4,2,1,0:T(8,128)S(1)}, u32[]{:S(2)}, u32[]{:S(2)}) async-start(f32[8,1,1,256,64]{3,4,2,1,0:T(8,128)} %broadcast_in_dim.75), calls=%async_computation | async-start | bytes 1048576 | tf_op jit(solution)/shard_map/all_to_all | solution.py:13
  13.4 99.3 %all-reduce.5.cloned.1.call-start = ((), (), s32[]{:S(2)}) async-start(), calls=%async_computation.4 | async-start | bytes 6291456 | tf_op jit(solution)/shard_map/psum | solution.py:37
  21.5 91.2 %copy-start.8 = (f32[4,1,256,16]{2,3,1,0:T(8,128)S(1)}, f32[4,1,256,16]{2,3,1,0:T(8,128)}, u32[]{:S(2)}) copy-start(f32[4,1,256,16]{2,3,1,0:T(8,128)} %param.9) | copy-start | bytes 196612
  21.5 173.9 %all-reduce.7.cloned.1.call-start = ((), (), s32[]{:S(2)}) async-start(), calls=%async_computation.5 | async-start | bytes 6291456 | tf_op jit(solution)/shard_map/psum | solution.py:37
  112.7 141.0 %all-gather.6.cloned.1.call-start = ((), (), s32[]{:S(2)}) async-start(), calls=%async_computation.1 | async-start | bytes 2359296 | tf_op jit(solution)/shard_map/all_gather | solution.py:30
  122.9 160.1 %all-gather.10.cloned.1.call-start = ((), (), s32[]{:S(2)}) async-start(), calls=%async_computation.3 | async-start | bytes 2359296 | tf_op jit(solution)/shard_map/all_gather | solution.py:42
  196.5 48.1 %copy-start.3 = (f32[256,1024]{1,0:T(8,128)S(1)}, f32[256,1024]{1,0:T(8,128)}, u32[]{:S(2)}) copy-start(f32[256,1024]{1,0:T(8,128)} %get-tuple-element.91) | copy-start | bytes 3145732
  224.7 22.9 %copy-start.9 = (s32[2,2]{1,0:T(2,128)}, s32[2,2]{1,0:T(2,128)S(1)}, u32[]{:S(2)}) copy-start(s32[2,2]{1,0:T(2,128)S(1)} %get-tuple-element.347) | copy-start | bytes 52
  244.6 2.0 copy-start.4
  244.6 2.0 copy-start.6
  253.7 65.7 %all-gather.8.cloned.1.call-start = ((), (), s32[]{:S(2)}) async-start(), calls=%async_computation.2 | async-start | bytes 4718592 | tf_op jit(solution)/shard_map/all_gather | solution.py:42
  379.9 4.4 %copy-start.7 = (f32[2,128,128]{1,2,0:T(8,128)S(1)}, f32[2,128,128]{1,2,0:T(8,128)}, u32[]{:S(2)}) copy-start(f32[2,128,128]{1,2,0:T(8,128)} %custom-call.11) | copy-start | bytes 393220
  384.7 0.6 copy-start
  389.6 3.0 copy-start.1
  389.6 3.0 copy-start.5
Sparse Core Ops, SparseCore 0:
  21.6 91.0 all-reduce.4
  115.2 80.1 all-reduce.6
  197.2 36.2 all-gather.5
  253.8 29.1 all-gather.9
  284.7 34.5 all-gather.7
where the time goes:
time: 408 us; the launch traced here: 403 us
  waiting for transfers between devices  224 us (55%)
  other arithmetic  90 us (22%)
  local copies, waits for them, and re-layouts  40 us (10%)
  matrix products  19.9 us (5%)
  between operations  13.5 us (3%)
  blocking collectives  10.1 us (2%)
  starting transfers between devices  5.25 us (1%)
    psum x2, waiting for transfers between devices, broadcast_by_axis(): x = lax.psum(x, axis)  164 us
    all_gather x2, waiting for transfers between devices, picked(): lax.all_gather(x, axis)  58.4 us
    another operation x3, other arithmetic, solve_right(): jax.scipy.linalg.solve_triangular(diag_block, owned_cols.T, lower=True)  42.3 us
    another operation x4, other arithmetic, solve_left(): return jax.scipy.linalg.solve_triangular(diag_block, owned_rows, lower=True)  40.6 us
    another operation x12, local copies, waits for them, and re-layouts, solve_right(): jax.scipy.linalg.solve_triangular(diag_block, owned_cols.T, lower=True)  12.6 us
    all_gather x1, blocking collectives, gathered_by_axis(): nearer = lax.all_gather(x, axes[-1], axis=dim, tiled=True)  10.1 us
    another operation x25, local copies, waits for them, and re-layouts, solve_left(): return jax.scipy.linalg.solve_triangular(diag_block, owned_rows, lower=True)  8.39 us
  transfers between devices with their start and end apart: 6, of which 5 were waited for; matrix products, arithmetic and copies ran while one was open for 17% of the time, Pallas kernels for 0%

commit v1 on v0

v1 whole, which is shorter than its diff:
```python
import functools

import jax
import jax.numpy as jnp
from jax import lax
from jax.experimental import pallas as pl
from jax.experimental.pallas import tpu as pltpu
from jax.sharding import PartitionSpec as P

BS = 256
NX = 4
NZ = 8
NY = 4
CUT = 512
MESH = pl.DeviceIdType.MESH


def mm(a, b):
    return jnp.dot(a, b, precision=lax.Precision.HIGHEST, preferred_element_type=jnp.float32)


def tri_inverse(t):
    n, b = t.shape[0], 32
    rows = lax.broadcasted_iota(jnp.int32, (n, n), 0)
    cols = lax.broadcasted_iota(jnp.int32, (n, n), 1)
    t = jnp.where(rows >= cols, t, 0.0)
    same = (rows >> 5) == (cols >> 5)
    wide = (
        (lax.broadcasted_iota(jnp.int32, (b, n), 1) & (b - 1)) == lax.broadcasted_iota(jnp.int32, (b, n), 0)
    ).astype(jnp.float32)
    tall = (
        (lax.broadcasted_iota(jnp.int32, (n, b), 0) & (b - 1)) == lax.broadcasted_iota(jnp.int32, (n, b), 1)
    ).astype(jnp.float32)
    blocks = mm(jnp.where(same, t, 0.0), tall).reshape(n // b, b, b)
    bi = lax.broadcasted_iota(jnp.int32, (n // b, b, b), 1)
    bj = lax.broadcasted_iota(jnp.int32, (n // b, b, b), 2)
    diag = jnp.sum(jnp.where(bi == bj, blocks, 0.0), axis=2, keepdims=True)
    rdiag = 1.0 / diag
    lower = jnp.where(bi > bj, blocks * rdiag, 0.0)
    inv = jnp.where(bi == bj, rdiag, 0.0)
    for j in range(b - 1):
        inv = inv - lower[:, :, j : j + 1] * inv[:, j : j + 1, :]
    full = jnp.where(same, mm(inv.reshape(n, b), wide), 0.0)
    for shift in (5, 6, 7):
        off = ((rows >> (shift + 1)) == (cols >> (shift + 1))) & ((rows >> shift) != (cols >> shift))
        full = full - mm(mm(full, jnp.where(off, t, 0.0)), full)
    return full


def kernel(s_ref, l_ref, r_ref, o_ref, rt, st, tx, lt, yb, send_sem, recv_sem, sc_send, tc_send, sc_recv):
    me = lax.axis_index("prow")
    col = lax.axis_index("pcol")
    z, x = me // NX, me % NX
    y, c = col // 2, col % 2
    own = me

    def at_x(k):
        return (z * NX + (x + k + NX) % NX, col)

    def at_z(k):
        return (((z + k + NZ) % NZ) * NX + x, col)

    def at_y(k):
        return (me, ((y + k + NY) % NY) * 2 + c)

    partner = (me, y * 2 + 1 - c)

    barrier = pltpu.get_barrier_semaphore()
    near = [at_x(1), at_x(-1), at_x(2), at_z(1), at_z(-1), at_y(1), at_y(-1), at_y(2), partner]
    for dev in near:
        pl.semaphore_signal(barrier, inc=1, device_id=dev, device_id_type=MESH)
    for root in range(2):

        @pl.when(me != root)
        def _():
            pl.semaphore_signal(barrier, inc=1, device_id=(root, col), device_id_type=MESH)

    rt[z, x] = r_ref[...].T
    lt[col] = l_ref[...].T
    pl.semaphore_wait(barrier, jnp.where(me < 2, len(near) + NZ * NX - 1, len(near)))

    events = []

    def send(src, dst, dev):
        k = len(events)
        copy = pltpu.make_async_remote_copy(
            src_ref=src, dst_ref=dst, send_sem=send_sem.at[k], recv_sem=recv_sem.at[k], device_id=dev, device_id_type=MESH
        )
        copy.start()
        events.append(copy)
        return copy

    def same(ref, dev):
        return send(ref, ref, dev)

    def s_copy(root, dest):
        return pltpu.make_async_remote_copy(
            src_ref=s_ref.at[pl.ds(dest * 8, 8), :],
            dst_ref=st.at[dest // NX, dest % NX, pl.ds(root * 8, 8), :],
            send_sem=sc_send.at[dest],
            recv_sem=sc_recv.at[root],
            device_id=(dest, col),
            device_id_type=MESH,
        )

    def t_copy(root, k):
        dest = root * 16 + k
        return pltpu.make_async_remote_copy(
            src_ref=lt.at[col, pl.ds((k % 8) * 8, 8), pl.ds((k // 8) * 128, 128)],
            dst_ref=tx.at[col, dest // NX, dest % NX],
            send_sem=tc_send.at[k],
            recv_sem=sc_recv.at[2],
            device_id=(dest, col),
            device_id_type=MESH,
        )

    for root in range(2):

        @pl.when(me == root)
        def _():
            def t_body(k, carry):
                @pl.when(root * 16 + k != root)
                def _():
                    t_copy(root, k).start()

                return carry

            lax.fori_loop(0, 16, t_body, 0)

            def s_body(dest, carry):
                @pl.when(dest != root)
                def _():
                    s_copy(root, dest).start()

                return carry

            lax.fori_loop(0, NZ * NX, s_body, 0)
            st[root // NX, root % NX, root * 8 : root * 8 + 8, :] = s_ref[root * 8 : root * 8 + 8, :]

    @pl.when(me == 0)
    def _():
        tx[col, 0, 0] = lt[col, 0:8, 0:128]

    ca, cb = slice(0, CUT), slice(CUT, 1024)

    class Across:
        def __init__(self, view, plus, minus):
            self.view, self.most = view, {1: plus, -1: minus}
            self.rows = {}

        def first(self):
            self.xs = [same(self.view(z, x), at_x(k)) for k in (1, -1, 2)]

        def step(self, s):
            if s == 1:
                for e in self.xs:
                    e.wait_recv()
            for d in (1, -1):
                if s > 1 and (d, s - 1) in self.rows:
                    self.rows[d, s - 1].wait_recv()
                if s <= self.most[d]:
                    src = (z - d * (s - 1) + NZ) % NZ
                    self.rows[d, s] = same(self.view(src, None), at_z(d))

    class Along:
        def __init__(self, view, plus, minus):
            self.view, self.most = view, {1: plus, -1: minus}
            self.zs, self.xs, self.fs = {}, {}, []

        def to_x(self, key, src, d):
            self.xs[key] = (src, d, {k: same(self.view(src, x), at_x(k)) for k in (1, -1)})

        def first(self):
            for d in (1, -1):
                self.zs[d, 1] = same(self.view(z, x), at_z(d))
            self.to_x((1, 1), z, 1 if self.most[1] == 4 else -1)

        def step(self, s):
            for d in (1, -1):
                if s > 1 and (d, s - 1) in self.zs:
                    self.zs[d, s - 1].wait_recv()
                    src = (z - d * (s - 1) + NZ) % NZ
                    if s <= self.most[d]:
                        self.zs[d, s] = same(self.view(src, x), at_z(d))
                    self.to_x((d, s), src, d if s < 5 else -d)
            for d in (1, -1):
                if (d, s - 1) in self.xs:
                    self.forward((d, s - 1))

        def forward(self, key):
            src, d, sent = self.xs[key]
            sent[1].wait_recv()
            sent[-1].wait_recv()
            self.fs.append(same(self.view(src, (x - d + NX) % NX), at_x(d)))

        def last(self):
            for e in self.fs:
                e.wait_recv()

    def columns(ref, cut):
        def view(zz, xx):
            return ref.at[zz, :, :, cut] if xx is None else ref.at[zz, xx, :, cut]

        return view

    r_a = Across(columns(rt, ca), 4, 3)
    r_b = Along(columns(rt, cb), 4, 3)
    s_a = Across(columns(st, ca), 3, 4)
    s_b = Along(columns(st, cb), 3, 4)
    t_a = Across(lambda zz, xx: tx.at[col, zz] if xx is None else tx.at[col, zz, xx], 4, 3)

    class Panel:
        def __init__(self, ref):
            self.ref = ref

        def first(self):
            self.es = [same(self.ref.at[col], at_y(k)) for k in (1, -1, 2)]
            self.ps = [same(self.ref.at[col], partner)]

        def step(self):
            for k, e in zip((1, -1, 2), self.es):
                e.wait_recv()
                self.ps.append(same(self.ref.at[((y - k + NY) % NY) * 2 + c], partner))

        def last(self):
            for e in self.ps:
                e.wait_recv()

    l_p, t_p = Panel(lt), Panel(tx)

    l_p.first()
    r_a.first()
    r_b.first()

    @pl.when(me != 0)
    def _():
        t_copy(0, 0).wait_recv()

    t_a.first()
    r_a.step(1)
    l_p.step()
    t_a.step(1)
    r_b.step(2)
    r_a.step(2)
    t_a.step(2)

    @pl.when(me != 0)
    def _():
        s_copy(0, 0).wait_recv()

    @pl.when(me != 1)
    def _():
        s_copy(1, 0).wait_recv()

    s_a.first()
    s_b.first()
    r_b.step(3)
    t_a.step(3)
    r_a.step(3)
    s_a.step(1)
    s_b.step(2)
    t_a.step(4)
    r_b.step(4)
    r_a.step(4)
    t_a.step(5)
    t_p.first()
    s_a.step(2)
    s_b.step(3)
    r_b.step(5)
    r_a.step(5)
    t_p.step()
    s_a.step(3)
    s_b.step(4)
    r_b.step(6)
    s_a.step(4)
    s_b.step(5)
    r_b.last()
    s_a.step(5)
    s_b.step(6)
    s_b.last()
    l_p.last()
    t_p.last()

    def panel_of(root):
        halves = [tx[:, 4 * root + 2 * h : 4 * root + 2 * h + 2].reshape(512, 128) for h in range(2)]
        return jnp.concatenate(halves, axis=1)

    left0 = panel_of(0)
    left1 = panel_of(1)
    inv0 = tri_inverse(left0[0:BS].T)
    inv1 = tri_inverse(left1[BS:].T)
    t10 = left1[0:BS].T
    mine = lt[...].reshape(512, BS).T
    ri = lax.broadcasted_iota(jnp.int32, (BS, 512), 0)
    ci = lax.broadcasted_iota(jnp.int32, (BS, 512), 1)
    unit = jnp.where(ci == ri + me * BS, -1.0, 0.0)
    a = jnp.where(me < 2, unit, mine)
    w1 = mm(a[:, BS:], inv1)
    w0 = mm(a[:, :BS] - mm(w1, t10), inv0)
    base = jnp.where(me < 2, 0.0, s_ref[...])
    o_ref[...] = base - mm(w0, st[:, :, 0:8, :].reshape(BS, 1024)) - mm(w1, st[:, :, 8:16, :].reshape(BS, 1024))

    y_up = [
        pltpu.make_async_remote_copy(
            src_ref=yb.at[c],
            dst_ref=yb.at[c],
            send_sem=send_sem.at[len(events) + k],
            recv_sem=recv_sem.at[len(events) + 3],
            device_id=(me, k * 2 + c),
            device_id_type=MESH,
        )
        for k in (1, 2, 3)
    ]
    y_over = pltpu.make_async_remote_copy(
        src_ref=yb.at[c],
        dst_ref=yb.at[c],
        send_sem=send_sem.at[len(events) + 4],
        recv_sem=recv_sem.at[len(events) + 4],
        device_id=partner,
        device_id_type=MESH,
    )

    @pl.when(y == 0)
    def _():
        block = rt[pl.ds(4 * c, 4), :, :, 0:BS].reshape(BS, BS)
        yinv = tri_inverse(block.T).T

        @pl.when(c == 1)
        def _():
            y_over.wait_recv()
            o_ref[:, 0:BS] = o_ref[:, 0:BS] - mm(yb[0], rt[0:4, :, :, 0:BS].reshape(BS, BS))

        yb[c] = mm(o_ref[:, 0:BS], yinv)
        y_over.start()
        for e in y_up:
            e.start()

    @pl.when(y != 0)
    def _():
        y_up[0].wait_recv()
        y_over.start()

    @pl.when((y != 0) | (c == 0))
    def _():
        y_over.wait_recv()

    def right(cut):
        return o_ref[:, cut] - mm(yb[0], rt[0:4, :, :, cut].reshape(BS, -1)) - mm(yb[1], rt[4:8, :, :, cut].reshape(BS, -1))

    o_ref[:, 256:1024] = right(slice(256, 1024))

    @pl.when(y == 0)
    def _():
        o_ref[:, 0:BS] = yb[c]

    @pl.when(y != 0)
    def _():
        o_ref[:, 0:BS] = right(slice(0, 256))

    for e in events:
        e.wait_send()
    y_over.wait_send()

    @pl.when(y == 0)
    def _():
        for e in y_up:
            e.wait_send()

    for root in range(2):

        @pl.when(me == root)
        def _():
            def t_body(k, carry):
                @pl.when(root * 16 + k != root)
                def _():
                    t_copy(root, k).wait_send()

                return carry

            lax.fori_loop(0, 16, t_body, 0)

            def s_body(dest, carry):
                @pl.when(dest != root)
                def _():
                    s_copy(root, dest).wait_send()

                return carry

            lax.fori_loop(0, NZ * NX, s_body, 0)


N_EVENTS = 120


def shards(cross_cov, left_factor, right_factor):
    f32 = jnp.float32
    out = pl.pallas_call(
        kernel,
        out_shape=jax.ShapeDtypeStruct((BS, 1024), f32),
        in_specs=[pl.BlockSpec(memory_space=pltpu.VMEM)] * 3,
        out_specs=pl.BlockSpec(memory_space=pltpu.VMEM),
        scratch_shapes=[
            pltpu.VMEM((NZ, NX, 16, 1024), f32),
            pltpu.VMEM((NZ, NX, 16, 1024), f32),
            pltpu.VMEM((8, NZ, NX, 8, 128), f32),
            pltpu.VMEM((8, 64, 256), f32),
            pltpu.VMEM((2, BS, BS), f32),
            pltpu.SemaphoreType.DMA((N_EVENTS,)),
            pltpu.SemaphoreType.DMA((N_EVENTS,)),
            pltpu.SemaphoreType.DMA((NZ * NX,)),
            pltpu.SemaphoreType.DMA((16,)),
            pltpu.SemaphoreType.DMA((3,)),
        ],
        compiler_params=pltpu.CompilerParams(collective_id=0, has_side_effects=True, vmem_limit_bytes=60 * 1024 * 1024),
    )(
        cross_cov.reshape(BS, 1024),
        left_factor.reshape(BS, 64),
        right_factor.reshape(1024, 16),
    )
    return out.reshape(cross_cov.shape)


def solution(mesh):
    return jax.shard_map(
        shards,
        mesh=mesh,
        in_specs=(
            P(None, "prow", None, None, "pcol", None),
            P(None, "prow", None, "pcol"),
            P(None, "pcol", None, "prow"),
        ),
        out_specs=P(None, "prow", None, None, "pcol", None),
        check_vma=False,
    )
```

time: 408 us -> 114 us (0.28)
  the two profiles are of different devices: /device:TPU:151 before, /device:TPU:16 now
where the time goes in v1:
time: 114 us; the launch traced here: 113 us
  Pallas kernels  102 us (89%)
  local copies, waits for them, and re-layouts  7.25 us (6%)
  other arithmetic  3.96 us (3%)
    pallas_call x1, Pallas kernels, shards(): pl.pallas_call(kernel, out_shape=jax.ShapeDtypeStruct((BS, 1024), f32), i...  102 us
    unnamed x1, other arithmetic  3.96 us
    unnamed x5, local copies, waits for them, and re-layouts  3.8 us
    reshape x1, local copies, waits for them, and re-layouts, shards(): return out.reshape(cross_cov.shape)  3.44 us

profile of v1, /device:TPU:16, one launch (start us, length us, event | category | flops | bytes accessed | tf_op | source)
XLA Modules:
  0.0 113.3 jit_solution(17875720869989155354)
XLA Ops:
  0.0 0.0 copy-start
  0.0 1.6 %copy.4 = f32[1,1,256,64]{3,2,1,0:T(8,128)} copy(f32[1,1,256,64]{2,3,1,0:T(8,128)} %param.4) | data formatting | bytes 131072 | tf_op args[1]
  1.6 0.0 copy-done
  1.6 1.0 copy.5
  2.6 4.0 %reduce = f32[256,4,256]{2,1,0:T(4,128)S(1)} reduce(f32[1,1,256,4,1,256]{5,4,3,2,1,0:T(1,128)} %param.3, f32[]{:T(128)} %constant.3), dimensions={0,1,4}, to_apply=%param.3.reduce_sub_computation | reduce | bytes 2097156 | tf_op args[0]
  6.6 1.2 %copy.7 = f32[32,8,4,256]{3,1,2,0:T(8,128)} copy(f32[32,8,4,256]{3,2,1,0:T(4,128)S(1)} %bitcast.4) | data formatting | bytes 2097152
  7.8 102.1 %shard_map.37 = f32[256,1024]{1,0:T(8,128)} custom-call(f32[256,1024]{1,0:T(8,128)} %bitcast.5, f32[256,64]{1,0:T(8,128)} %bitcast.7, f32[1024,16]{1,0:T(8,128)} %bitcast.6), custom_call_target="tpu_custom_call" | custom-call | tf_op jit(solution)/shard_map/pallas_call | solution.py:397
  109.9 3.4 %reshape.16 = f32[1,1,256,4,1,256]{5,4,3,2,1,0:T(1,128)} reshape(f32[256,1024]{1,0:T(8,128)} %shard_map.37) | data formatting | bytes 2097152 | tf_op jit(solution)/shard_map/reshape | solution.py:420
Async XLA Ops:
  0.0 1.6 %copy-start = (f32[4,1,256,16]{2,3,1,0:T(8,128)S(1)}, f32[4,1,256,16]{2,3,1,0:T(8,128)}, u32[]{:S(2)}) copy-start(f32[4,1,256,16]{2,3,1,0:T(8,128)} %param.5) | copy-start | bytes 196612

commit v2 on v1

--- a/solution.py
+++ b/solution.py
@@ -47,7 +47,7 @@
     return full
 
 
-def kernel(s_ref, l_ref, r_ref, o_ref, rt, st, tx, lt, yb, send_sem, recv_sem, sc_send, tc_send, sc_recv):
+def kernel(s_hbm, l_ref, r_ref, o_hbm, s_ref, o_ref, rt, st, tx, lt, yb, io_sem, send_sem, recv_sem, sc_send, tc_send, sc_recv):
     me = lax.axis_index("prow")
     col = lax.axis_index("pcol")
     z, x = me // NX, me % NX
@@ -65,6 +65,14 @@
 
     partner = (me, y * 2 + 1 - c)
 
+    s_in = [
+        pltpu.make_async_copy(s_hbm.at[:, h, :], s_ref.at[:, h * 128 : (h + 1) * 128], io_sem.at[h]) for h in range(8)
+    ]
+    o_out = [
+        pltpu.make_async_copy(o_ref.at[:, h * 128 : (h + 1) * 128], o_hbm.at[:, h, :], io_sem.at[8 + h]) for h in range(8)
+    ]
+    for e in s_in:
+        e.start()
     barrier = pltpu.get_barrier_semaphore()
     near = [at_x(1), at_x(-1), at_x(2), at_z(1), at_z(-1), at_y(1), at_y(-1), at_y(2), partner]
     for dev in near:
@@ -75,10 +83,12 @@
         def _():
             pl.semaphore_signal(barrier, inc=1, device_id=(root, col), device_id_type=MESH)
 
-    rt[z, x] = r_ref[...].T
-    lt[col] = l_ref[...].T
+    rt[z, x] = r_ref[...]
+    lt[col] = l_ref[...]
     pl.semaphore_wait(barrier, jnp.where(me < 2, len(near) + NZ * NX - 1, len(near)))
 
+    for e in s_in:
+        e.wait()
     events = []
 
     def send(src, dst, dev):
@@ -141,7 +151,6 @@
     def _():
         tx[col, 0, 0] = lt[col, 0:8, 0:128]
 
-    ca, cb = slice(0, CUT), slice(CUT, 1024)
 
     class Across:
         def __init__(self, view, plus, minus):
@@ -197,16 +206,24 @@
             for e in self.fs:
                 e.wait_recv()
 
-    def columns(ref, cut):
+    def blocks(first):
         def view(zz, xx):
-            return ref.at[zz, :, :, cut] if xx is None else ref.at[zz, xx, :, cut]
+            return rt.at[zz, :, first : first + 2] if xx is None else rt.at[zz, xx, first : first + 2]
 
         return view
 
-    r_a = Across(columns(rt, ca), 4, 3)
-    r_b = Along(columns(rt, cb), 4, 3)
-    s_a = Across(columns(st, ca), 3, 4)
-    s_b = Along(columns(st, cb), 3, 4)
+    def columns(first):
+        cut = slice(first, first + 512)
+
+        def view(zz, xx):
+            return st.at[zz, :, :, cut] if xx is None else st.at[zz, xx, :, cut]
+
+        return view
+
+    r_a = Across(blocks(0), 4, 3)
+    r_b = Along(blocks(2), 4, 3)
+    s_a = Across(columns(0), 3, 4)
+    s_b = Along(columns(512), 3, 4)
     t_a = Across(lambda zz, xx: tx.at[col, zz] if xx is None else tx.at[col, zz, xx], 4, 3)
 
     class Panel:
@@ -322,13 +339,13 @@
 
     @pl.when(y == 0)
     def _():
-        block = rt[pl.ds(4 * c, 4), :, :, 0:BS].reshape(BS, BS)
+        block = rt[pl.ds(4 * c, 4), :, 0].reshape(BS, BS)
         yinv = tri_inverse(block.T).T
 
         @pl.when(c == 1)
         def _():
             y_over.wait_recv()
-            o_ref[:, 0:BS] = o_ref[:, 0:BS] - mm(yb[0], rt[0:4, :, :, 0:BS].reshape(BS, BS))
+            o_ref[:, 0:BS] = o_ref[:, 0:BS] - mm(yb[0], rt[0:4, :, 0].reshape(BS, BS))
 
         yb[c] = mm(o_ref[:, 0:BS], yinv)
         y_over.start()
@@ -344,10 +361,16 @@
     def _():
         y_over.wait_recv()
 
-    def right(cut):
-        return o_ref[:, cut] - mm(yb[0], rt[0:4, :, :, cut].reshape(BS, -1)) - mm(yb[1], rt[4:8, :, :, cut].reshape(BS, -1))
-
-    o_ref[:, 256:1024] = right(slice(256, 1024))
+    def right(d):
+        cut = slice(d * BS, (d + 1) * BS)
+        o_ref[:, cut] = (
+            o_ref[:, cut] - mm(yb[0], rt[0:4, :, d].reshape(BS, BS)) - mm(yb[1], rt[4:8, :, d].reshape(BS, BS))
+        )
+
+    for d in (1, 2, 3):
+        right(d)
+        o_out[2 * d].start()
+        o_out[2 * d + 1].start()
 
     @pl.when(y == 0)
     def _():
@@ -355,7 +378,10 @@
 
     @pl.when(y != 0)
     def _():
-        o_ref[:, 0:BS] = right(slice(0, 256))
+        right(0)
+
+    o_out[0].start()
+    o_out[1].start()
 
     for e in events:
         e.wait_send()
@@ -388,6 +414,9 @@
 
             lax.fori_loop(0, NZ * NX, s_body, 0)
 
+    for e in o_out:
+        e.wait()
+
 
 N_EVENTS = 120
 
@@ -396,15 +425,22 @@
     f32 = jnp.float32
     out = pl.pallas_call(
         kernel,
-        out_shape=jax.ShapeDtypeStruct((BS, 1024), f32),
-        in_specs=[pl.BlockSpec(memory_space=pltpu.VMEM)] * 3,
-        out_specs=pl.BlockSpec(memory_space=pltpu.VMEM),
+        out_shape=jax.ShapeDtypeStruct((BS, 8, 128), f32),
+        in_specs=[
+            pl.BlockSpec(memory_space=pl.ANY),
+            pl.BlockSpec(memory_space=pltpu.VMEM),
+            pl.BlockSpec(memory_space=pltpu.VMEM),
+        ],
+        out_specs=pl.BlockSpec(memory_space=pl.ANY),
         scratch_shapes=[
-            pltpu.VMEM((NZ, NX, 16, 1024), f32),
+            pltpu.VMEM((BS, 1024), f32),
+            pltpu.VMEM((BS, 1024), f32),
+            pltpu.VMEM((NZ, NX, 4, 16, BS), f32),
             pltpu.VMEM((NZ, NX, 16, 1024), f32),
             pltpu.VMEM((8, NZ, NX, 8, 128), f32),
             pltpu.VMEM((8, 64, 256), f32),
             pltpu.VMEM((2, BS, BS), f32),
+            pltpu.SemaphoreType.DMA((16,)),
             pltpu.SemaphoreType.DMA((N_EVENTS,)),
             pltpu.SemaphoreType.DMA((N_EVENTS,)),
             pltpu.SemaphoreType.DMA((NZ * NX,)),
@@ -413,9 +449,9 @@
         ],
         compiler_params=pltpu.CompilerParams(collective_id=0, has_side_effects=True, vmem_limit_bytes=60 * 1024 * 1024),
     )(
-        cross_cov.reshape(BS, 1024),
-        left_factor.reshape(BS, 64),
-        right_factor.reshape(1024, 16),
+        cross_cov.reshape(BS, 8, 128),
+        left_factor.reshape(BS, 64).T,
+        jnp.swapaxes(right_factor.reshape(4, BS, 16), 1, 2),
     )
     return out.reshape(cross_cov.shape)
 

time: 114 us -> 105 us (0.921)
  local copies, waits for them, and re-layouts: 7.25 us -> 2.91 us
  other arithmetic: 3.96 us -> 0 us
    unnamed x1 -> x0, other arithmetic: 3.96 us -> none
    reshape x1 -> x0, local copies, waits for them, and re-layouts: 3.44 us -> none  [shards(): return out.reshape(cross_cov.shape)]
    unnamed x5 -> x1, local copies, waits for them, and re-layouts: 3.8 us -> 2.91 us
where the time goes in v2:
time: 105 us
  Pallas kernels  102 us (97%)
  local copies, waits for them, and re-layouts  2.91 us (3%)
    pallas_call x1, Pallas kernels, shards(): pl.pallas_call(kernel, out_shape=jax.ShapeDtypeStruct((BS, 8, 128), f32),...  102 us
    unnamed x1, local copies, waits for them, and re-layouts  2.91 us

profile of v2, /device:TPU:16, one launch (start us, length us, event | category | flops | bytes accessed | tf_op | source)
XLA Modules:
  0.0 104.7 jit_solution(13883378432390986280)
XLA Ops:
  0.0 101.7 %shard_map.37 = f32[256,8,128]{2,1,0:T(8,128)} custom-call(f32[256,8,128]{2,1,0:T(8,128)} %bitcast.9, f32[64,256]{1,0:T(8,128)} %bitcast.10, f32[4,16,256]{2,1,0:T(8,128)} %bitcast.11), custom_call_target="tpu_custom_call" | custom-call | tf_op jit(solution)/shard_map/pallas_call | solution.py:426
  101.8 2.9 %copy.6 = f32[1,1,256,4,1,256]{5,4,3,2,1,0:T(1,128)} copy(f32[1,1,256,4,1,256]{5,4,3,2,1,0:T(1,128)} %bitcast.8) | data formatting | bytes 2097152

commit v3 on v2

v3 whole, which is shorter than its diff:
```python
import functools

import jax
import jax.numpy as jnp
from jax import lax
from jax.experimental import pallas as pl
from jax.experimental.pallas import tpu as pltpu
from jax.sharding import PartitionSpec as P

BS = 256
NX = 4
NZ = 8
NY = 4
R_CUT = 2
MESH = pl.DeviceIdType.MESH


def mm(a, b):
    return jnp.dot(a, b, precision=lax.Precision.HIGHEST, preferred_element_type=jnp.float32)


def inverse_stages(ts, result):
    n, b = ts[0].shape[0], 32
    m = n // b
    rows = lax.broadcasted_iota(jnp.int32, (n, n), 0)
    cols = lax.broadcasted_iota(jnp.int32, (n, n), 1)
    same = (rows >> 5) == (cols >> 5)
    wide = (
        (lax.broadcasted_iota(jnp.int32, (b, n), 1) & (b - 1)) == lax.broadcasted_iota(jnp.int32, (b, n), 0)
    ).astype(jnp.float32)
    tall = (
        (lax.broadcasted_iota(jnp.int32, (n, b), 0) & (b - 1)) == lax.broadcasted_iota(jnp.int32, (n, b), 1)
    ).astype(jnp.float32)
    ts = [jnp.where(rows >= cols, t, 0.0) for t in ts]
    blocks = jnp.concatenate([mm(jnp.where(same, t, 0.0), tall).reshape(m, b, b) for t in ts], axis=0)
    bi = lax.broadcasted_iota(jnp.int32, blocks.shape, 1)
    bj = lax.broadcasted_iota(jnp.int32, blocks.shape, 2)
    diag = jnp.sum(jnp.where(bi == bj, blocks, 0.0), axis=2, keepdims=True)
    rdiag = 1.0 / diag
    lower = jnp.where(bi > bj, blocks * rdiag, 0.0)
    inv = jnp.where(bi == bj, rdiag, 0.0)
    yield
    for j in range(b - 1):
        inv = inv - lower[:, :, j : j + 1] * inv[:, j : j + 1, :]
        if j == b // 2:
            yield
    fulls = [jnp.where(same, mm(inv[k * m : k * m + m].reshape(n, b), wide), 0.0) for k in range(len(ts))]
    yield
    for shift in (5, 6, 7):
        off = ((rows >> (shift + 1)) == (cols >> (shift + 1))) & ((rows >> shift) != (cols >> shift))
        parts = [mm(full, jnp.where(off, t, 0.0)) for full, t in zip(fulls, ts)]
        fulls = [full - mm(part, full) for full, part in zip(fulls, parts)]
        yield
    result.extend(fulls)


def kernel(s_hbm, l_ref, r_ref, o_hbm, s_ref, o_ref, rt, st, tx, lt, yb, io_sem, send_sem, recv_sem, sh_send, s_send, s_recv, t_send, t_recv, y_send, y_recv):
    me = lax.axis_index("prow")
    col = lax.axis_index("pcol")
    z, x = me // NX, me % NX
    y, c = col // 2, col % 2

    def at_x(k):
        return (z * NX + (x + k + NX) % NX, col)

    def at_z(k):
        return (((z + k + NZ) % NZ) * NX + x, col)

    def at_y(k):
        return (me, ((y + k + NY) % NY) * 2 + c)

    partner = (me, y * 2 + 1 - c)

    s_in = [
        pltpu.make_async_copy(s_hbm.at[:, h, :], s_ref.at[:, h * 128 : (h + 1) * 128], io_sem.at[h]) for h in range(8)
    ]
    o_out = [
        pltpu.make_async_copy(o_ref.at[:, h * 128 : (h + 1) * 128], o_hbm.at[:, h, :], io_sem.at[8 + h]) for h in range(8)
    ]
    for e in s_in:
        e.start()
    barrier = pltpu.get_barrier_semaphore()
    near = [at_x(1), at_x(-1), at_x(2), at_z(1), at_z(-1), at_y(1), at_y(-1), at_y(2), partner]
    for dev in near:
        pl.semaphore_signal(barrier, inc=1, device_id=dev, device_id_type=MESH)
    rt[z, x] = r_ref[...]
    lt[col] = l_ref[...]
    pl.semaphore_wait(barrier, len(near))

    for e in s_in:
        e.wait()
    for root in range(2):

        @pl.when(me == root)
        def _():
            st[root, root * 4 : root * 4 + 4] = s_ref[:, root * BS : (root + 1) * BS].reshape(4, 64, BS)
            tx[col, root, root * 16 : root * 16 + 16] = l_ref[root * 16 : root * 16 + 16]

    events = []

    def send(src, dst, dev):
        k = len(events)
        copy = pltpu.make_async_remote_copy(
            src_ref=src, dst_ref=dst, send_sem=send_sem.at[k], recv_sem=recv_sem.at[k], device_id=dev, device_id_type=MESH
        )
        copy.start()
        events.append(copy)
        return copy

    def same(ref, dev):
        return send(ref, ref, dev)

    def remote(src, dst, ssem, rsem, dev):
        return pltpu.make_async_remote_copy(
            src_ref=src, dst_ref=dst, send_sem=ssem, recv_sem=rsem, device_id=dev, device_id_type=MESH
        )

    dist = jnp.where(z <= NZ // 2, z, NZ - z)
    zdir = jnp.where(z <= NZ // 2, 1, -1)
    passes_on = ((z >= 1) & (z <= 3)) | (z >= 6)

    def s_share(root, k, d):
        return remote(
            s_ref.at[pl.ds(k * 64, 64), pl.ds(d * BS, BS)],
            st.at[d, root * 4 + k],
            sh_send.at[k * 4 + d],
            s_recv.at[0, root * 4 + k],
            (d, col),
        )

    def s_along(k, d, which):
        return remote(st.at[x, k], st.at[x, k], s_send.at[which, k], s_recv.at[0, k], at_z(d))

    def s_across(k, which):
        return remote(st.at[x, k], st.at[x, k], s_send.at[2 + which, k], s_recv.at[1 + which, k], at_x(1 - 2 * which))

    def s_over(k):
        d = 1 - 2 * (k % 2)
        part = st.at[(x - d + NX) % NX, k]
        return remote(part, part, s_send.at[4, k], s_recv.at[3, k], at_x(d))

    def s_slot(j):
        turn = j - dist

        @pl.when((turn >= 0) & (turn < 8))
        def _():
            k = turn // 2 + 4 * (turn % 2)

            @pl.when((z != 0) | (x != k // 4))
            def _():
                s_along(k, 1, 0).wait_recv()

            @pl.when(z == 0)
            def _():
                s_along(k, 1, 0).start()
                s_along(k, -1, 1).start()

            @pl.when(passes_on)
            def _():
                s_along(k, zdir, 0).start()

            s_across(k, 0).start()
            s_across(k, 1).start()

        @pl.when((turn >= 1) & (turn < 9))
        def _():
            k = (turn - 1) // 2 + 4 * ((turn - 1) % 2)
            s_across(k, 0).wait_recv()
            s_across(k, 1).wait_recv()
            s_over(k).start()

    def s_end():
        for k in range(8):
            s_over(k).wait_recv()

    def s_sent():
        @pl.when((z == 0) | passes_on)
        def _():
            for k in range(8):
                s_along(k, 1, 0).wait_send()

        @pl.when(z == 0)
        def _():
            for k in range(8):
                s_along(k, -1, 1).wait_send()

        for k in range(8):
            s_across(k, 0).wait_send()
            s_across(k, 1).wait_send()
            s_over(k).wait_send()

    def t_share(root, d):
        return remote(
            l_ref.at[pl.ds(d * 16, 16)],
            tx.at[col, root, pl.ds(d * 16, 16)],
            t_send.at[d],
            t_recv.at[root],
            (d, col),
        )

    quarter = tx.at[col, :, pl.ds(x * 16, 16)]
    t_along = [remote(quarter, quarter, t_send.at[4 + w], t_recv.at[2], at_z(d)) for w, d in enumerate((1, -1, zdir))]
    t_across = [remote(quarter, quarter, t_send.at[7 + w], t_recv.at[3 + w], at_x(d)) for w, d in enumerate((1, -1, 2))]
    t_up = [remote(tx.at[col], tx.at[col], t_send.at[10 + w], t_recv.at[6 + w], at_y(d)) for w, d in enumerate((1, -1, 2))]

    def t_over(w):
        part = tx.at[((y - (0, 1, -1, 2)[w] + NY) % NY) * 2 + c]
        return remote(part, part, t_send.at[13 + w], t_recv.at[9 + w], partner)

    def t_slot(n):
        @pl.when(dist == n)
        def _():
            if n == 0:
                for root in range(2):

                    @pl.when(x != root)
                    def _():
                        t_share(root, x).wait_recv()

                t_along[0].start()
                t_along[1].start()
            else:
                t_along[2].wait_recv()

                @pl.when(passes_on)
                def _():
                    t_along[2].start()

            for e in t_across:
                e.start()

        @pl.when(dist == n - 1)
        def _():
            for e in t_across:
                e.wait_recv()
            for e in t_up:
                e.start()
            t_over(0).start()

    def t_step():
        for w in range(3):
            t_up[w].wait_recv()
            t_over(w + 1).start()

    def t_end():
        for w in range(4):
            t_over(w).wait_recv()

    def t_sent():
        @pl.when(z == 0)
        def _():
            t_along[0].wait_send()
            t_along[1].wait_send()

        @pl.when(passes_on)
        def _():
            t_along[2].wait_send()

        for e in t_across + t_up + [t_over(w) for w in range(4)]:
            e.wait_send()

    def t_shares():
        for root in range(2):

            @pl.when(me == root)
            def _():
                for d in range(NX):
                    if d != root:
                        t_share(root, d).start()

    def s_shares(k):
        for root in range(2):

            @pl.when(me == root)
            def _():
                for d in range(NX):
                    if d != root:
                        s_share(root, k, d).start()

    def shares_sent():
        for root in range(2):

            @pl.when(me == root)
            def _():
                for d in range(NX):
                    if d != root:
                        t_share(root, d).wait_send()
                        for k in range(4):
                            s_share(root, k, d).wait_send()

    class Across:
        def __init__(self, view, plus, minus):
            self.view, self.most = view, {1: plus, -1: minus}
            self.sent = {}

        def on(self, d, s, off):
            src = (z - d * (s - 1) + NZ) % NZ
            self.sent[d, s, off] = same(self.view(src, (x + off + NX) % NX), at_z(d))

        def first(self):
            self.xs = [same(self.view(z, x), at_x(k)) for k in (1, -1, 2)]
            for d in (1, -1):
                self.on(d, 1, 0)

        def step(self, s):
            if s == 1:
                for e, k in zip(self.xs, (1, -1, 2)):
                    e.wait_recv()
                    for d in (1, -1):
                        self.on(d, 1, -k)
                return
            for off in (0, -1, 1, -2):
                for d in (1, -1):
                    if (d, s - 1, off) in self.sent:
                        self.sent[d, s - 1, off].wait_recv()
                    if s <= self.most[d]:
                        self.on(d, s, off)

    class Along:
        def __init__(self, view, plus, minus):
            self.view, self.most = view, {1: plus, -1: minus}
            self.zs, self.xs, self.fs = {}, {}, []

        def to_x(self, key, src, d):
            self.xs[key] = (src, d, {k: same(self.view(src, x), at_x(k)) for k in (1, -1)})

        def first(self):
            for d in (1, -1):
                self.zs[d, 1] = same(self.view(z, x), at_z(d))
            self.to_x((1, 1), z, 1 if self.most[1] == 4 else -1)

        def step(self, s):
            for d in (1, -1):
                if s > 1 and (d, s - 1) in self.zs:
                    self.zs[d, s - 1].wait_recv()
                    src = (z - d * (s - 1) + NZ) % NZ
                    if s <= self.most[d]:
                        self.zs[d, s] = same(self.view(src, x), at_z(d))
                    self.to_x((d, s), src, d if s < 5 else -d)
            for d in (1, -1):
                if (d, s - 1) in self.xs:
                    self.forward((d, s - 1))

        def forward(self, key):
            src, d, sent = self.xs[key]
            sent[1].wait_recv()
            sent[-1].wait_recv()
            self.fs.append(same(self.view(src, (x - d + NX) % NX), at_x(d)))

        def last(self):
            for e in self.fs:
                e.wait_recv()

    def blocks(first, number):
        def view(zz, xx):
            return rt.at[zz, xx, first : first + number]

        return view

    r_a = Across(blocks(0, R_CUT), 4, 3)
    r_b = Along(blocks(R_CUT, 4 - R_CUT), 4, 3)

    class Panel:
        def __init__(self, ref):
            self.ref = ref

        def first(self):
            self.es = [same(self.ref.at[col], at_y(k)) for k in (1, -1, 2)]
            self.ps = [same(self.ref.at[col], partner)]

        def step(self):
            for k, e in zip((1, -1, 2), self.es):
                e.wait_recv()
                self.ps.append(same(self.ref.at[((y - k + NY) % NY) * 2 + c], partner))

        def last(self):
            for e in self.ps:
                e.wait_recv()

    l_p = Panel(lt)

    def panel_of(root):
        return tx[:, root].reshape(512, BS)

    t_shares()
    r_a.first()
    r_b.first()
    l_p.first()
    t_slot(0)
    s_shares(0)
    r_a.step(1)
    r_b.step(2)
    s_shares(1)
    t_slot(1)
    s_slot(0)
    s_shares(2)
    r_b.step(3)
    r_a.step(2)
    s_shares(3)
    t_slot(2)
    s_slot(1)
    r_b.step(4)
    t_slot(3)
    s_slot(2)
    r_a.step(3)
    t_slot(4)
    r_b.step(5)
    s_slot(3)
    t_slot(5)
    r_a.step(4)
    r_b.step(6)
    l_p.step()
    t_step()
    s_slot(4)
    l_p.last()
    t_end()
    left0 = panel_of(0)
    left1 = panel_of(1)
    x_inv = []
    x_stages = inverse_stages([left0[0:BS].T, left1[BS:].T], x_inv)
    next(x_stages)
    r_a.step(5)
    y_inv = []
    y_stages = inverse_stages([rt[pl.ds(4 * c, 4), :, 0].reshape(BS, BS).T], y_inv)
    s_slot(5)
    next(x_stages)
    next(y_stages)
    s_slot(6)
    next(x_stages)
    s_slot(7)
    next(x_stages)
    next(y_stages)
    s_slot(8)
    next(x_stages)
    next(y_stages)
    s_slot(9)
    next(x_stages)
    next(y_stages)
    s_slot(10)
    for _ in x_stages:
        pass
    next(y_stages)
    s_slot(11)
    for _ in y_stages:
        pass
    s_slot(12)
    r_b.last()
    s_end()
    inv0, inv1 = x_inv
    for _ in y_stages:
        pass
    t10 = left1[0:BS].T
    mine = lt[...].reshape(512, BS).T
    ri = lax.broadcasted_iota(jnp.int32, (BS, 512), 0)
    ci = lax.broadcasted_iota(jnp.int32, (BS, 512), 1)
    unit = jnp.where(ci == ri + me * BS, -1.0, 0.0)
    a = jnp.where(me < 2, unit, mine)
    w1 = mm(a[:, BS:], inv1)
    w0 = mm(a[:, :BS] - mm(w1, t10), inv0)

    def left(d):
        cut = slice(d * BS, (d + 1) * BS)
        base = jnp.where(me < 2, 0.0, s_ref[:, cut])
        o_ref[:, cut] = (
            base - mm(w0, st[d, 0:4].reshape(BS, BS)) - mm(w1, st[d, 4:8].reshape(BS, BS))
        )

    left(0)

    def y_copy(half, dev, k, over):
        part = yb.at[c, pl.ds(half * 128, 128)]
        return pltpu.make_async_remote_copy(
            src_ref=part,
            dst_ref=part,
            send_sem=y_send.at[k],
            recv_sem=y_recv.at[2 * over + half],
            device_id=dev,
            device_id_type=MESH,
        )

    over = [y_copy(h, partner, h, 1) for h in range(2)]
    along = [y_copy(0, at_y(1), 2, 0), y_copy(1, at_y(-1), 3, 0), y_copy(1, at_y(1), 4, 0), y_copy(0, at_y(-1), 5, 0)]

    @pl.when(y == 0)
    def _():
        @pl.when(c == 1)
        def _():
            for e in over:
                e.wait_recv()
            o_ref[:, 0:BS] = o_ref[:, 0:BS] - mm(yb[0], rt[0:4, :, 0].reshape(BS, BS))

        yb[c] = mm(o_ref[:, 0:BS], y_inv[0].T)
        for e in over:
            e.start()
        for e in along:
            e.start()

    for d in (1, 2, 3):
        left(d)

    @pl.when(y == 1)
    def _():
        along[0].wait_recv()
        along[0].start()
        over[0].start()
        along[1].wait_recv()
        over[1].start()

    @pl.when(y == 3)
    def _():
        along[1].wait_recv()
        along[1].start()
        over[1].start()
        along[0].wait_recv()
        over[0].start()

    @pl.when(y == 2)
    def _():
        along[0].wait_recv()
        over[0].start()
        along[1].wait_recv()
        over[1].start()

    @pl.when((y != 0) | (c == 0))
    def _():
        for e in over:
            e.wait_recv()

    def right(d):
        cut = slice(d * BS, (d + 1) * BS)
        o_ref[:, cut] = (
            o_ref[:, cut] - mm(yb[0], rt[0:4, :, d].reshape(BS, BS)) - mm(yb[1], rt[4:8, :, d].reshape(BS, BS))
        )

    for d in (1, 2, 3):
        right(d)
        o_out[2 * d].start()
        o_out[2 * d + 1].start()

    @pl.when(y == 0)
    def _():
        o_ref[:, 0:BS] = yb[c]

    @pl.when(y != 0)
    def _():
        right(0)

    o_out[0].start()
    o_out[1].start()

    for e in events:
        e.wait_send()
    for e in over:
        e.wait_send()

    @pl.when((y == 0) | (y == 1))
    def _():
        along[0].wait_send()

    @pl.when((y == 0) | (y == 3))
    def _():
        along[1].wait_send()

    @pl.when(y == 0)
    def _():
        along[2].wait_send()
        along[3].wait_send()

    s_sent()
    t_sent()
    shares_sent()
    for e in o_out:
        e.wait()


N_EVENTS = 80


def shards(cross_cov, left_factor, right_factor):
    f32 = jnp.float32
    out = pl.pallas_call(
        kernel,
        out_shape=jax.ShapeDtypeStruct((BS, 8, 128), f32),
        in_specs=[
            pl.BlockSpec(memory_space=pl.ANY),
            pl.BlockSpec(memory_space=pltpu.VMEM),
            pl.BlockSpec(memory_space=pltpu.VMEM),
        ],
        out_specs=pl.BlockSpec(memory_space=pl.ANY),
        scratch_shapes=[
            pltpu.VMEM((BS, 1024), f32),
            pltpu.VMEM((BS, 1024), f32),
            pltpu.VMEM((NZ, NX, 4, 16, BS), f32),
            pltpu.VMEM((4, 8, 64, BS), f32),
            pltpu.VMEM((8, 2, 64, BS), f32),
            pltpu.VMEM((8, 64, 256), f32),
            pltpu.VMEM((2, BS, BS), f32),
            pltpu.SemaphoreType.DMA((16,)),
            pltpu.SemaphoreType.DMA((N_EVENTS,)),
            pltpu.SemaphoreType.DMA((N_EVENTS,)),
            pltpu.SemaphoreType.DMA((16,)),
            pltpu.SemaphoreType.DMA((5, 8)),
            pltpu.SemaphoreType.DMA((4, 8)),
            pltpu.SemaphoreType.DMA((17,)),
            pltpu.SemaphoreType.DMA((13,)),
            pltpu.SemaphoreType.DMA((6,)),
            pltpu.SemaphoreType.DMA((4,)),
        ],
        compiler_params=pltpu.CompilerParams(collective_id=0, has_side_effects=True, vmem_limit_bytes=60 * 1024 * 1024),
    )(
        cross_cov.reshape(BS, 8, 128),
        left_factor.reshape(BS, 64).T,
        jnp.swapaxes(right_factor.reshape(4, BS, 16), 1, 2),
    )
    return out.reshape(cross_cov.shape)


def solution(mesh):
    return jax.shard_map(
        shards,
        mesh=mesh,
        in_specs=(
            P(None, "prow", None, None, "pcol", None),
            P(None, "prow", None, "pcol"),
            P(None, "pcol", None, "prow"),
        ),
        out_specs=P(None, "prow", None, None, "pcol", None),
        check_vma=False,
    )
```

time: 105 us -> 86.4 us (0.82)
  the two profiles are of different devices: /device:TPU:16 before, /device:TPU:151 now
where the time goes in v3:
time: 86.4 us; the launch traced here: 85 us
  Pallas kernels  82.1 us (95%)
  local copies, waits for them, and re-layouts  2.91 us (3%)
    pallas_call x1, Pallas kernels, shards(): pl.pallas_call(kernel, out_shape=jax.ShapeDtypeStruct((BS, 8, 128), f32),...  82.1 us
    unnamed x1, local copies, waits for them, and re-layouts  2.91 us

profile of v3, /device:TPU:151, one launch (start us, length us, event | category | flops | bytes accessed | tf_op | source)
XLA Modules:
  0.0 85.0 jit_solution(5052888431453655295)
XLA Ops:
  0.0 82.1 %shard_map.37 = f32[256,8,128]{2,1,0:T(8,128)} custom-call(f32[256,8,128]{2,1,0:T(8,128)} %bitcast.9, f32[64,256]{1,0:T(8,128)} %bitcast.10, f32[4,16,256]{2,1,0:T(8,128)} %bitcast.11), custom_call_target="tpu_custom_call" | custom-call | tf_op jit(solution)/shard_map/pallas_call | solution.py:581
  82.1 2.9 %copy.6 = f32[1,1,256,4,1,256]{5,4,3,2,1,0:T(1,128)} copy(f32[1,1,256,4,1,256]{5,4,3,2,1,0:T(1,128)} %bitcast.8) | data formatting | bytes 2097152

commit v4 on v3

--- a/solution.py
+++ b/solution.py
@@ -12,11 +12,26 @@
 NZ = 8
 NY = 4
 R_CUT = 2
+LAG = 2
 MESH = pl.DeviceIdType.MESH
 
 
 def mm(a, b):
     return jnp.dot(a, b, precision=lax.Precision.HIGHEST, preferred_element_type=jnp.float32)
+
+
+def halves(a):
+    high = a.astype(jnp.bfloat16)
+    return high, (a - high.astype(jnp.float32)).astype(jnp.bfloat16)
+
+
+def mm3(a, b):
+    (ah, al), (bh, bl) = a, b
+
+    def dot(p, q):
+        return jnp.dot(p, q, preferred_element_type=jnp.float32)
+
+    return dot(ah, bh) + (dot(ah, bl) + dot(al, bh))
 
 
 def inverse_stages(ts, result):
@@ -54,7 +69,7 @@
     result.extend(fulls)
 
 
-def kernel(s_hbm, l_ref, r_ref, o_hbm, s_ref, o_ref, rt, st, tx, lt, yb, io_sem, send_sem, recv_sem, sh_send, s_send, s_recv, t_send, t_recv, y_send, y_recv):
+def kernel(s_hbm, l_ref, r_ref, o_hbm, s_ref, o_ref, rt, st, tx, lt, yb, xv, rh, rl, io_sem, send_sem, recv_sem, sh_send, s_send, s_recv, t_send, t_recv, y_send, y_recv):
     me = lax.axis_index("prow")
     col = lax.axis_index("pcol")
     z, x = me // NX, me % NX
@@ -74,17 +89,19 @@
     s_in = [
         pltpu.make_async_copy(s_hbm.at[:, h, :], s_ref.at[:, h * 128 : (h + 1) * 128], io_sem.at[h]) for h in range(8)
     ]
-    o_out = [
-        pltpu.make_async_copy(o_ref.at[:, h * 128 : (h + 1) * 128], o_hbm.at[:, h, :], io_sem.at[8 + h]) for h in range(8)
-    ]
+
+    def write(d, value):
+        for h in range(2):
+            o_hbm[pl.ds(2 * d + h, BS, stride=8), :] = value[:, h * 128 : (h + 1) * 128]
+
+    s_in.append(pltpu.make_async_copy(l_ref, lt.at[col], io_sem.at[16]))
+    s_in.append(pltpu.make_async_copy(r_ref, rt.at[z, x], io_sem.at[17]))
     for e in s_in:
         e.start()
     barrier = pltpu.get_barrier_semaphore()
     near = [at_x(1), at_x(-1), at_x(2), at_z(1), at_z(-1), at_y(1), at_y(-1), at_y(2), partner]
     for dev in near:
         pl.semaphore_signal(barrier, inc=1, device_id=dev, device_id_type=MESH)
-    rt[z, x] = r_ref[...]
-    lt[col] = l_ref[...]
     pl.semaphore_wait(barrier, len(near))
 
     for e in s_in:
@@ -94,7 +111,7 @@
         @pl.when(me == root)
         def _():
             st[root, root * 4 : root * 4 + 4] = s_ref[:, root * BS : (root + 1) * BS].reshape(4, 64, BS)
-            tx[col, root, root * 16 : root * 16 + 16] = l_ref[root * 16 : root * 16 + 16]
+            tx[col, root, root * 16 : root * 16 + 16] = lt[col, root * 16 : root * 16 + 16]
 
     events = []
 
@@ -139,6 +156,13 @@
         part = st.at[(x - d + NX) % NX, k]
         return remote(part, part, s_send.at[4, k], s_recv.at[3, k], at_x(d))
 
+    def feeds(k):
+        return z == 1 + (NZ - 2) * ((k // 2 + k) % 2)
+
+    def s_back(k):
+        part = st.at[(x + 2) % NX, k]
+        return remote(part, part, s_send.at[5, k], s_recv.at[3, k], (x, col))
+
     def s_slot(j):
         turn = j - dist
 
@@ -159,19 +183,47 @@
             def _():
                 s_along(k, zdir, 0).start()
 
-            s_across(k, 0).start()
-            s_across(k, 1).start()
-
-        @pl.when((turn >= 1) & (turn < 9))
+            @pl.when(z != 0)
+            def _():
+                s_across(k, 0).start()
+                s_across(k, 1).start()
+
+        if LAG <= j < LAG + 8:
+
+            @pl.when(z == 0)
+            def _():
+                k = (j - LAG) // 2 + 4 * ((j - LAG) % 2)
+                s_across(k, 0).start()
+                s_across(k, 1).start()
+
+        @pl.when((turn >= 1) & (turn < 9) & (z != 0))
         def _():
             k = (turn - 1) // 2 + 4 * ((turn - 1) % 2)
             s_across(k, 0).wait_recv()
             s_across(k, 1).wait_recv()
             s_over(k).start()
 
+        @pl.when((turn >= 2) & (turn < 10) & (dist == 1))
+        def _():
+            k = (turn - 2) // 2 + 4 * ((turn - 2) % 2)
+
+            @pl.when(feeds(k))
+            def _():
+                s_over(k).wait_recv()
+                s_back(k).start()
+
     def s_end():
+        @pl.when(z == 0)
+        def _():
+            for k in range(8):
+                s_across(k, 0).wait_recv()
+                s_across(k, 1).wait_recv()
+
         for k in range(8):
-            s_over(k).wait_recv()
+
+            @pl.when(jnp.logical_not(feeds(k)))
+            def _():
+                s_over(k).wait_recv()
 
     def s_sent():
         @pl.when((z == 0) | passes_on)
@@ -187,11 +239,18 @@
         for k in range(8):
             s_across(k, 0).wait_send()
             s_across(k, 1).wait_send()
-            s_over(k).wait_send()
+
+            @pl.when(z != 0)
+            def _():
+                s_over(k).wait_send()
+
+            @pl.when(feeds(k))
+            def _():
+                s_back(k).wait_send()
 
     def t_share(root, d):
         return remote(
-            l_ref.at[pl.ds(d * 16, 16)],
+            lt.at[col, pl.ds(d * 16, 16)],
             tx.at[col, root, pl.ds(d * 16, 16)],
             t_send.at[d],
             t_recv.at[root],
@@ -337,9 +396,11 @@
                     if s <= self.most[d]:
                         self.zs[d, s] = same(self.view(src, x), at_z(d))
                     self.to_x((d, s), src, d if s < 5 else -d)
+
+        def cross(self, s):
             for d in (1, -1):
-                if (d, s - 1) in self.xs:
-                    self.forward((d, s - 1))
+                if (d, s) in self.xs:
+                    self.forward((d, s))
 
         def forward(self, key):
             src, d, sent = self.xs[key]
@@ -387,68 +448,61 @@
     r_b.first()
     l_p.first()
     t_slot(0)
-    s_shares(0)
+    for k in range(4):
+        s_shares(k)
     r_a.step(1)
     r_b.step(2)
-    s_shares(1)
     t_slot(1)
     s_slot(0)
-    s_shares(2)
     r_b.step(3)
     r_a.step(2)
-    s_shares(3)
     t_slot(2)
     s_slot(1)
+    r_b.cross(1)
     r_b.step(4)
     t_slot(3)
     s_slot(2)
     r_a.step(3)
+    r_b.cross(2)
     t_slot(4)
+    s_slot(3)
     r_b.step(5)
-    s_slot(3)
     t_slot(5)
+    s_slot(4)
+    r_b.cross(3)
     r_a.step(4)
-    r_b.step(6)
     l_p.step()
+    s_slot(5)
     t_step()
-    s_slot(4)
+    r_b.cross(4)
+    r_b.cross(5)
     l_p.last()
     t_end()
-    left0 = panel_of(0)
-    left1 = panel_of(1)
-    x_inv = []
-    x_stages = inverse_stages([left0[0:BS].T, left1[BS:].T], x_inv)
-    next(x_stages)
     r_a.step(5)
-    y_inv = []
-    y_stages = inverse_stages([rt[pl.ds(4 * c, 4), :, 0].reshape(BS, BS).T], y_inv)
-    s_slot(5)
-    next(x_stages)
-    next(y_stages)
+    pair = []
+    stages = inverse_stages(
+        [tx[pl.ds(4 * c, 4), c].reshape(BS, BS).T, rt[pl.ds(4 * c, 4), :, 0].reshape(BS, BS).T], pair
+    )
+    next(stages)
     s_slot(6)
-    next(x_stages)
+    next(stages)
     s_slot(7)
-    next(x_stages)
-    next(y_stages)
+    next(stages)
     s_slot(8)
-    next(x_stages)
-    next(y_stages)
+    next(stages)
     s_slot(9)
-    next(x_stages)
-    next(y_stages)
+    next(stages)
     s_slot(10)
-    for _ in x_stages:
+    for _ in stages:
         pass
-    next(y_stages)
+    xv[c] = pair[0]
+    xv_copy = same(xv.at[c], partner)
     s_slot(11)
-    for _ in y_stages:
-        pass
     s_slot(12)
     r_b.last()
-    s_end()
-    inv0, inv1 = x_inv
-    for _ in y_stages:
-        pass
+    left1 = panel_of(1)
+    xv_copy.wait_recv()
+    inv0, inv1 = xv[0], xv[1]
     t10 = left1[0:BS].T
     mine = lt[...].reshape(512, BS).T
     ri = lax.broadcasted_iota(jnp.int32, (BS, 512), 0)
@@ -458,13 +512,14 @@
     w1 = mm(a[:, BS:], inv1)
     w0 = mm(a[:, :BS] - mm(w1, t10), inv0)
 
+    wide = halves(jnp.concatenate([w0, w1], axis=1))
+
     def left(d):
         cut = slice(d * BS, (d + 1) * BS)
         base = jnp.where(me < 2, 0.0, s_ref[:, cut])
-        o_ref[:, cut] = (
-            base - mm(w0, st[d, 0:4].reshape(BS, BS)) - mm(w1, st[d, 4:8].reshape(BS, BS))
-        )
-
+        o_ref[:, cut] = base - mm3(wide, halves(st[d].reshape(2 * BS, BS)))
+
+    s_end()
     left(0)
 
     def y_copy(half, dev, k, over):
@@ -489,7 +544,7 @@
                 e.wait_recv()
             o_ref[:, 0:BS] = o_ref[:, 0:BS] - mm(yb[0], rt[0:4, :, 0].reshape(BS, BS))
 
-        yb[c] = mm(o_ref[:, 0:BS], y_inv[0].T)
+        yb[c] = mm(o_ref[:, 0:BS], pair[1].T)
         for e in over:
             e.start()
         for e in along:
@@ -497,6 +552,15 @@
 
     for d in (1, 2, 3):
         left(d)
+    for d in range(4):
+        high, low = halves(rt[:, :, d].reshape(2 * BS, BS))
+        rh[d] = high
+        rl[d] = low
+    for e in events:
+        e.wait_send()
+    s_sent()
+    t_sent()
+    shares_sent()
 
     @pl.when(y == 1)
     def _():
@@ -526,30 +590,22 @@
         for e in over:
             e.wait_recv()
 
+    both = halves(jnp.concatenate([yb[0], yb[1]], axis=1))
+
     def right(d):
-        cut = slice(d * BS, (d + 1) * BS)
-        o_ref[:, cut] = (
-            o_ref[:, cut] - mm(yb[0], rt[0:4, :, d].reshape(BS, BS)) - mm(yb[1], rt[4:8, :, d].reshape(BS, BS))
-        )
+        return o_ref[:, d * BS : (d + 1) * BS] - mm3(both, (rh[d], rl[d]))
 
     for d in (1, 2, 3):
-        right(d)
-        o_out[2 * d].start()
-        o_out[2 * d + 1].start()
+        write(d, right(d))
 
     @pl.when(y == 0)
     def _():
-        o_ref[:, 0:BS] = yb[c]
+        write(0, yb[c])
 
     @pl.when(y != 0)
     def _():
-        right(0)
-
-    o_out[0].start()
-    o_out[1].start()
-
-    for e in events:
-        e.wait_send()
+        write(0, right(0))
+
     for e in over:
         e.wait_send()
 
@@ -565,12 +621,6 @@
     def _():
         along[2].wait_send()
         along[3].wait_send()
-
-    s_sent()
-    t_sent()
-    shares_sent()
-    for e in o_out:
-        e.wait()
 
 
 N_EVENTS = 80
@@ -580,13 +630,13 @@
     f32 = jnp.float32
     out = pl.pallas_call(
         kernel,
-        out_shape=jax.ShapeDtypeStruct((BS, 8, 128), f32),
+        out_shape=jax.ShapeDtypeStruct((BS * 8, 128), f32),
         in_specs=[
-            pl.BlockSpec(memory_space=pl.ANY),
-            pl.BlockSpec(memory_space=pltpu.VMEM),
-            pl.BlockSpec(memory_space=pltpu.VMEM),
+            pl.BlockSpec(memory_space=pltpu.HBM),
+            pl.BlockSpec(memory_space=pltpu.HBM),
+            pl.BlockSpec(memory_space=pltpu.HBM),
         ],
-        out_specs=pl.BlockSpec(memory_space=pl.ANY),
+        out_specs=pl.BlockSpec(memory_space=pltpu.VMEM),
         scratch_shapes=[
             pltpu.VMEM((BS, 1024), f32),
             pltpu.VMEM((BS, 1024), f32),
@@ -595,18 +645,21 @@
             pltpu.VMEM((8, 2, 64, BS), f32),
             pltpu.VMEM((8, 64, 256), f32),
             pltpu.VMEM((2, BS, BS), f32),
-            pltpu.SemaphoreType.DMA((16,)),
+            pltpu.VMEM((2, BS, BS), f32),
+            pltpu.VMEM((4, 2 * BS, BS), jnp.bfloat16),
+            pltpu.VMEM((4, 2 * BS, BS), jnp.bfloat16),
+            pltpu.SemaphoreType.DMA((18,)),
             pltpu.SemaphoreType.DMA((N_EVENTS,)),
             pltpu.SemaphoreType.DMA((N_EVENTS,)),
             pltpu.SemaphoreType.DMA((16,)),
-            pltpu.SemaphoreType.DMA((5, 8)),
+            pltpu.SemaphoreType.DMA((6, 8)),
             pltpu.SemaphoreType.DMA((4, 8)),
             pltpu.SemaphoreType.DMA((17,)),
             pltpu.SemaphoreType.DMA((13,)),
             pltpu.SemaphoreType.DMA((6,)),
             pltpu.SemaphoreType.DMA((4,)),
         ],
-        compiler_params=pltpu.CompilerParams(collective_id=0, has_side_effects=True, vmem_limit_bytes=60 * 1024 * 1024),
+        compiler_params=pltpu.CompilerParams(collective_id=0, has_side_effects=True, vmem_limit_bytes=55000000),
     )(
         cross_cov.reshape(BS, 8, 128),
         left_factor.reshape(BS, 64).T,

time: 86.4 us -> 73.3 us (0.85)
  Pallas kernels: 82.1 us -> 69.8 us
    pallas_call x1, Pallas kernels: 82.1 us -> 69.8 us  [shards(): pl.pallas_call(kernel, out_shape=jax.ShapeDtypeStruct((BS * 8, 128), f32)...]
    unnamed x1 -> x5, local copies, waits for them, and re-layouts: 2.91 us -> 2.65 us
where the time goes in v4:
time: 73.3 us; the launch traced here: 72.4 us
  Pallas kernels  69.8 us (95%)
  local copies, waits for them, and re-layouts  2.65 us (4%)
    pallas_call x1, Pallas kernels, shards(): pl.pallas_call(kernel, out_shape=jax.ShapeDtypeStruct((BS * 8, 128), f32)...  69.8 us
    unnamed x5, local copies, waits for them, and re-layouts  2.65 us

profile of v4, /device:TPU:151, one launch (start us, length us, event | category | flops | bytes accessed | tf_op | source)
XLA Modules:
  0.0 72.4 jit_solution(11431727168146294264)
XLA Ops:
  0.0 0.0 copy-start
  0.0 0.8 %copy-done = f32[1,1,256,64]{2,3,1,0:T(8,128)S(1)} copy-done((f32[1,1,256,64]{2,3,1,0:T(8,128)S(1)}, f32[1,1,256,64]{2,3,1,0:T(8,128)}, u32[]{:S(2)}) %copy-start) | copy-done | bytes 65560
  0.8 0.0 copy-start.1
  0.8 0.8 %copy-done.1 = f32[4,1,256,16]{2,3,1,0:T(8,128)S(1)} copy-done((f32[4,1,256,16]{2,3,1,0:T(8,128)S(1)}, f32[4,1,256,16]{2,3,1,0:T(8,128)}, u32[]{:S(2)}) %copy-start.1) | copy-done | bytes 65560
  1.7 69.8 %shard_map.37 = f32[2048,128]{1,0:T(8,128)S(1)} custom-call(f32[256,8,128]{2,1,0:T(8,128)} %bitcast.11, f32[64,256]{1,0:T(8,128)S(1)} %bitcast.9, f32[4,16,256]{2,1,0:T(8,128)S(1)} %bitcast.10), custom_call_target="tpu_custom_call" | custom-call | tf_op jit(solution)/shard_map/pallas_call | solution.py:631
  71.5 1.0 %copy.6 = f32[1,1,256,4,1,256]{5,4,3,2,1,0:T(1,128)} copy(f32[1,1,256,4,1,256]{5,4,3,2,1,0:T(1,128)S(1)} %bitcast.8) | data formatting | bytes 2097152
Async XLA Ops:
  0.0 0.8 %copy-start = (f32[1,1,256,64]{2,3,1,0:T(8,128)S(1)}, f32[1,1,256,64]{2,3,1,0:T(8,128)}, u32[]{:S(2)}) copy-start(f32[1,1,256,64]{2,3,1,0:T(8,128)} %param.4) | copy-start | bytes 196612
  0.8 0.8 %copy-start.1 = (f32[4,1,256,16]{2,3,1,0:T(8,128)S(1)}, f32[4,1,256,16]{2,3,1,0:T(8,128)}, u32[]{:S(2)}) copy-start(f32[4,1,256,16]{2,3,1,0:T(8,128)} %param.5) | copy-start | bytes 196612

commit v5 on v4

--- a/solution.py
+++ b/solution.py
@@ -87,15 +87,15 @@
     partner = (me, y * 2 + 1 - c)
 
     s_in = [
-        pltpu.make_async_copy(s_hbm.at[:, h, :], s_ref.at[:, h * 128 : (h + 1) * 128], io_sem.at[h]) for h in range(8)
+        pltpu.make_async_copy(s_hbm.at[:, h, :], s_ref.at[:, h * 128 : (h + 1) * 128], io_sem.at[0]) for h in range(8)
     ]
 
     def write(d, value):
         for h in range(2):
             o_hbm[pl.ds(2 * d + h, BS, stride=8), :] = value[:, h * 128 : (h + 1) * 128]
 
-    s_in.append(pltpu.make_async_copy(l_ref, lt.at[col], io_sem.at[16]))
-    s_in.append(pltpu.make_async_copy(r_ref, rt.at[z, x], io_sem.at[17]))
+    s_in.append(pltpu.make_async_copy(l_ref, lt.at[col], io_sem.at[1]))
+    s_in.append(pltpu.make_async_copy(r_ref, rt.at[z, x], io_sem.at[2]))
     for e in s_in:
         e.start()
     barrier = pltpu.get_barrier_semaphore()
@@ -104,8 +104,9 @@
         pl.semaphore_signal(barrier, inc=1, device_id=dev, device_id_type=MESH)
     pl.semaphore_wait(barrier, len(near))
 
-    for e in s_in:
-        e.wait()
+    pltpu.make_async_copy(s_ref, s_ref, io_sem.at[0]).wait()
+    s_in[8].wait()
+    s_in[9].wait()
     for root in range(2):
 
         @pl.when(me == root)
@@ -115,17 +116,21 @@
 
     events = []
 
-    def send(src, dst, dev):
-        k = len(events)
+    def same(ref, dev, group):
         copy = pltpu.make_async_remote_copy(
-            src_ref=src, dst_ref=dst, send_sem=send_sem.at[k], recv_sem=recv_sem.at[k], device_id=dev, device_id_type=MESH
+            src_ref=ref,
+            dst_ref=ref,
+            send_sem=send_sem.at[group],
+            recv_sem=recv_sem.at[len(events)],
+            device_id=dev,
+            device_id_type=MESH,
         )
         copy.start()
         events.append(copy)
         return copy
 
-    def same(ref, dev):
-        return send(ref, ref, dev)
+    def all_sent(sem, ref):
+        pltpu.make_async_copy(ref, ref, sem).wait()
 
     def remote(src, dst, ssem, rsem, dev):
         return pltpu.make_async_remote_copy(
@@ -140,28 +145,28 @@
         return remote(
             s_ref.at[pl.ds(k * 64, 64), pl.ds(d * BS, BS)],
             st.at[d, root * 4 + k],
-            sh_send.at[k * 4 + d],
+            sh_send.at[0],
             s_recv.at[0, root * 4 + k],
             (d, col),
         )
 
     def s_along(k, d, which):
-        return remote(st.at[x, k], st.at[x, k], s_send.at[which, k], s_recv.at[0, k], at_z(d))
+        return remote(st.at[x, k], st.at[x, k], s_send.at[which], s_recv.at[0, k], at_z(d))
 
     def s_across(k, which):
-        return remote(st.at[x, k], st.at[x, k], s_send.at[2 + which, k], s_recv.at[1 + which, k], at_x(1 - 2 * which))
+        return remote(st.at[x, k], st.at[x, k], s_send.at[2], s_recv.at[1, k], at_x(1 - 2 * which))
 
     def s_over(k):
         d = 1 - 2 * (k % 2)
         part = st.at[(x - d + NX) % NX, k]
-        return remote(part, part, s_send.at[4, k], s_recv.at[3, k], at_x(d))
+        return remote(part, part, s_send.at[3], s_recv.at[2, k], at_x(d))
 
     def feeds(k):
         return z == 1 + (NZ - 2) * ((k // 2 + k) % 2)
 
     def s_back(k):
         part = st.at[(x + 2) % NX, k]
-        return remote(part, part, s_send.at[5, k], s_recv.at[3, k], (x, col))
+        return remote(part, part, s_send.at[4], s_recv.at[2, k], (x, col))
 
     def s_slot(j):
         turn = j - dist
@@ -199,8 +204,7 @@
         @pl.when((turn >= 1) & (turn < 9) & (z != 0))
         def _():
             k = (turn - 1) // 2 + 4 * ((turn - 1) % 2)
-            s_across(k, 0).wait_recv()
-            s_across(k, 1).wait_recv()
+            all_sent(s_recv.at[1, k], st.at[0, 0:2])
             s_over(k).start()
 
         @pl.when((turn >= 2) & (turn < 10) & (dist == 1))
@@ -216,8 +220,7 @@
         @pl.when(z == 0)
         def _():
             for k in range(8):
-                s_across(k, 0).wait_recv()
-                s_across(k, 1).wait_recv()
+                all_sent(s_recv.at[1, k], st.at[0, 0:2])
 
         for k in range(8):
 
@@ -228,43 +231,39 @@
     def s_sent():
         @pl.when((z == 0) | passes_on)
         def _():
-            for k in range(8):
-                s_along(k, 1, 0).wait_send()
+            all_sent(s_send.at[0], st.at[0])
 
         @pl.when(z == 0)
         def _():
-            for k in range(8):
-                s_along(k, -1, 1).wait_send()
-
-        for k in range(8):
-            s_across(k, 0).wait_send()
-            s_across(k, 1).wait_send()
-
-            @pl.when(z != 0)
-            def _():
-                s_over(k).wait_send()
-
-            @pl.when(feeds(k))
-            def _():
-                s_back(k).wait_send()
+            all_sent(s_send.at[1], st.at[0])
+
+        all_sent(s_send.at[2], st.at[0:2])
+
+        @pl.when(z != 0)
+        def _():
+            all_sent(s_send.at[3], st.at[0])
+
+        @pl.when(dist == 1)
+        def _():
+            all_sent(s_send.at[4], st.at[0, 0:4])
 
     def t_share(root, d):
         return remote(
             lt.at[col, pl.ds(d * 16, 16)],
             tx.at[col, root, pl.ds(d * 16, 16)],
-            t_send.at[d],
+            t_send.at[0],
             t_recv.at[root],
             (d, col),
         )
 
     quarter = tx.at[col, :, pl.ds(x * 16, 16)]
-    t_along = [remote(quarter, quarter, t_send.at[4 + w], t_recv.at[2], at_z(d)) for w, d in enumerate((1, -1, zdir))]
-    t_across = [remote(quarter, quarter, t_send.at[7 + w], t_recv.at[3 + w], at_x(d)) for w, d in enumerate((1, -1, 2))]
-    t_up = [remote(tx.at[col], tx.at[col], t_send.at[10 + w], t_recv.at[6 + w], at_y(d)) for w, d in enumerate((1, -1, 2))]
+    t_along = [remote(quarter, quarter, t_send.at[1], t_recv.at[2], at_z(d)) for d in (1, -1, zdir)]
+    t_across = [remote(quarter, quarter, t_send.at[2], t_recv.at[3 + w], at_x(d)) for w, d in enumerate((1, -1, 2))]
+    t_up = [remote(tx.at[col], tx.at[col], t_send.at[3], t_recv.at[6 + w], at_y(d)) for w, d in enumerate((1, -1, 2))]
 
     def t_over(w):
         part = tx.at[((y - (0, 1, -1, 2)[w] + NY) % NY) * 2 + c]
-        return remote(part, part, t_send.at[13 + w], t_recv.at[9 + w], partner)
+        return remote(part, part, t_send.at[4], t_recv.at[9 + w], partner)
 
     def t_slot(n):
         @pl.when(dist == n)
@@ -308,15 +307,15 @@
     def t_sent():
         @pl.when(z == 0)
         def _():
-            t_along[0].wait_send()
-            t_along[1].wait_send()
+            all_sent(t_send.at[1], tx.at[0:2, :, 0:16])
 
         @pl.when(passes_on)
         def _():
-            t_along[2].wait_send()
-
-        for e in t_across + t_up + [t_over(w) for w in range(4)]:
-            e.wait_send()
+            all_sent(t_send.at[1], tx.at[0, :, 0:16])
+
+        all_sent(t_send.at[2], tx.at[0:3, :, 0:16])
+        all_sent(t_send.at[3], tx.at[0:3])
+        all_sent(t_send.at[4], tx.at[0:4])
 
     def t_shares():
         for root in range(2):
@@ -337,15 +336,10 @@
                         s_share(root, k, d).start()
 
     def shares_sent():
-        for root in range(2):
-
-            @pl.when(me == root)
-            def _():
-                for d in range(NX):
-                    if d != root:
-                        t_share(root, d).wait_send()
-                        for k in range(4):
-                            s_share(root, k, d).wait_send()
+        @pl.when(me < 2)
+        def _():
+            all_sent(t_send.at[0], lt.at[0, 0:48])
+            all_sent(sh_send.at[0], st.at[0:3, 0:4])
 
     class Across:
         def __init__(self, view, plus, minus):
@@ -354,10 +348,10 @@
 
         def on(self, d, s, off):
             src = (z - d * (s - 1) + NZ) % NZ
-            self.sent[d, s, off] = same(self.view(src, (x + off + NX) % NX), at_z(d))
+            self.sent[d, s, off] = same(self.view(src, (x + off + NX) % NX), at_z(d), 0)
 
         def first(self):
-            self.xs = [same(self.view(z, x), at_x(k)) for k in (1, -1, 2)]
+            self.xs = [same(self.view(z, x), at_x(k), 0) for k in (1, -1, 2)]
             for d in (1, -1):
                 self.on(d, 1, 0)
 
@@ -381,11 +375,11 @@
             self.zs, self.xs, self.fs = {}, {}, []
 
         def to_x(self, key, src, d):
-            self.xs[key] = (src, d, {k: same(self.view(src, x), at_x(k)) for k in (1, -1)})
+            self.xs[key] = (src, d, {k: same(self.view(src, x), at_x(k), 1) for k in (1, -1)})
 
         def first(self):
             for d in (1, -1):
-                self.zs[d, 1] = same(self.view(z, x), at_z(d))
+                self.zs[d, 1] = same(self.view(z, x), at_z(d), 1)
             self.to_x((1, 1), z, 1 if self.most[1] == 4 else -1)
 
         def step(self, s):
@@ -394,7 +388,7 @@
                     self.zs[d, s - 1].wait_recv()
                     src = (z - d * (s - 1) + NZ) % NZ
                     if s <= self.most[d]:
-                        self.zs[d, s] = same(self.view(src, x), at_z(d))
+                        self.zs[d, s] = same(self.view(src, x), at_z(d), 1)
                     self.to_x((d, s), src, d if s < 5 else -d)
 
         def cross(self, s):
@@ -406,7 +400,7 @@
             src, d, sent = self.xs[key]
             sent[1].wait_recv()
             sent[-1].wait_recv()
-            self.fs.append(same(self.view(src, (x - d + NX) % NX), at_x(d)))
+            self.fs.append(same(self.view(src, (x - d + NX) % NX), at_x(d), 1))
 
         def last(self):
             for e in self.fs:
@@ -426,13 +420,13 @@
             self.ref = ref
 
         def first(self):
-            self.es = [same(self.ref.at[col], at_y(k)) for k in (1, -1, 2)]
-            self.ps = [same(self.ref.at[col], partner)]
+            self.es = [same(self.ref.at[col], at_y(k), 2) for k in (1, -1, 2)]
+            self.ps = [same(self.ref.at[col], partner, 2)]
 
         def step(self):
             for k, e in zip((1, -1, 2), self.es):
                 e.wait_recv()
-                self.ps.append(same(self.ref.at[((y - k + NY) % NY) * 2 + c], partner))
+                self.ps.append(same(self.ref.at[((y - k + NY) % NY) * 2 + c], partner, 2))
 
         def last(self):
             for e in self.ps:
@@ -496,7 +490,7 @@
     for _ in stages:
         pass
     xv[c] = pair[0]
-    xv_copy = same(xv.at[c], partner)
+    xv_copy = same(xv.at[c], partner, 3)
     s_slot(11)
     s_slot(12)
     r_b.last()
@@ -556,8 +550,10 @@
         high, low = halves(rt[:, :, d].reshape(2 * BS, BS))
         rh[d] = high
         rl[d] = low
-    for e in events:
-        e.wait_send()
+    all_sent(send_sem.at[0], s_ref.at[0:248])
+    all_sent(send_sem.at[1], s_ref.at[0:248])
+    all_sent(send_sem.at[2], lt.at[0:7])
+    all_sent(send_sem.at[3], xv.at[0])
     s_sent()
     t_sent()
     shares_sent()
@@ -623,7 +619,7 @@
         along[3].wait_send()
 
 
-N_EVENTS = 80
+N_EVENTS = 70
 
 
 def shards(cross_cov, left_factor, right_factor):
@@ -648,13 +644,13 @@
             pltpu.VMEM((2, BS, BS), f32),
             pltpu.VMEM((4, 2 * BS, BS), jnp.bfloat16),
             pltpu.VMEM((4, 2 * BS, BS), jnp.bfloat16),
-            pltpu.SemaphoreType.DMA((18,)),
+            pltpu.SemaphoreType.DMA((3,)),
+            pltpu.SemaphoreType.DMA((4,)),
             pltpu.SemaphoreType.DMA((N_EVENTS,)),
-            pltpu.SemaphoreType.DMA((N_EVENTS,)),
-            pltpu.SemaphoreType.DMA((16,)),
-            pltpu.SemaphoreType.DMA((6, 8)),
-            pltpu.SemaphoreType.DMA((4, 8)),
-            pltpu.SemaphoreType.DMA((17,)),
+            pltpu.SemaphoreType.DMA((1,)),
+            pltpu.SemaphoreType.DMA((5,)),
+            pltpu.SemaphoreType.DMA((3, 8)),
+            pltpu.SemaphoreType.DMA((5,)),
             pltpu.SemaphoreType.DMA((13,)),
             pltpu.SemaphoreType.DMA((6,)),
             pltpu.SemaphoreType.DMA((4,)),

time: 73.3 us -> 71.6 us (0.977)
  Pallas kernels: 69.8 us -> 68 us
    pallas_call x1, Pallas kernels: 69.8 us -> 68 us  [shards(): pl.pallas_call(kernel, out_shape=jax.ShapeDtypeStruct((BS * 8, 128), f32)...]
where the time goes in v5:
time: 71.6 us; the launch traced here: 70.7 us
  Pallas kernels  68 us (95%)
  local copies, waits for them, and re-layouts  2.65 us (4%)
    pallas_call x1, Pallas kernels, shards(): pl.pallas_call(kernel, out_shape=jax.ShapeDtypeStruct((BS * 8, 128), f32)...  68 us
    unnamed x5, local copies, waits for them, and re-layouts  2.65 us

profile of v5, /device:TPU:151, one launch (start us, length us, event | category | flops | bytes accessed | tf_op | source)
XLA Modules:
  0.0 70.7 jit_solution(6816413395311287320)
XLA Ops:
  0.0 0.0 copy-start
  0.0 0.8 %copy-done = f32[1,1,256,64]{2,3,1,0:T(8,128)S(1)} copy-done((f32[1,1,256,64]{2,3,1,0:T(8,128)S(1)}, f32[1,1,256,64]{2,3,1,0:T(8,128)}, u32[]{:S(2)}) %copy-start) | copy-done | bytes 65560
  0.8 0.0 copy-start.1
  0.8 0.8 %copy-done.1 = f32[4,1,256,16]{2,3,1,0:T(8,128)S(1)} copy-done((f32[4,1,256,16]{2,3,1,0:T(8,128)S(1)}, f32[4,1,256,16]{2,3,1,0:T(8,128)}, u32[]{:S(2)}) %copy-start.1) | copy-done | bytes 65560
  1.7 68.0 %shard_map.37 = f32[2048,128]{1,0:T(8,128)S(1)} custom-call(f32[256,8,128]{2,1,0:T(8,128)} %bitcast.11, f32[64,256]{1,0:T(8,128)S(1)} %bitcast.9, f32[4,16,256]{2,1,0:T(8,128)S(1)} %bitcast.10), custom_call_target="tpu_custom_call" | custom-call | tf_op jit(solution)/shard_map/pallas_call | solution.py:627
  69.7 1.0 %copy.6 = f32[1,1,256,4,1,256]{5,4,3,2,1,0:T(1,128)} copy(f32[1,1,256,4,1,256]{5,4,3,2,1,0:T(1,128)S(1)} %bitcast.8) | data formatting | bytes 2097152
Async XLA Ops:
  0.0 0.8 %copy-start = (f32[1,1,256,64]{2,3,1,0:T(8,128)S(1)}, f32[1,1,256,64]{2,3,1,0:T(8,128)}, u32[]{:S(2)}) copy-start(f32[1,1,256,64]{2,3,1,0:T(8,128)} %param.4) | copy-start | bytes 196612
  0.8 0.8 %copy-start.1 = (f32[4,1,256,16]{2,3,1,0:T(8,128)S(1)}, f32[4,1,256,16]{2,3,1,0:T(8,128)}, u32[]{:S(2)}) copy-start(f32[4,1,256,16]{2,3,1,0:T(8,128)} %param.5) | copy-start | bytes 196612

commit v6 on v5

--- a/solution.py
+++ b/solution.py
@@ -201,15 +201,15 @@
                 s_across(k, 0).start()
                 s_across(k, 1).start()
 
-        @pl.when((turn >= 1) & (turn < 9) & (z != 0))
-        def _():
-            k = (turn - 1) // 2 + 4 * ((turn - 1) % 2)
+        @pl.when((turn >= 2) & (turn < 10) & (z != 0))
+        def _():
+            k = (turn - 2) // 2 + 4 * ((turn - 2) % 2)
             all_sent(s_recv.at[1, k], st.at[0, 0:2])
             s_over(k).start()
 
-        @pl.when((turn >= 2) & (turn < 10) & (dist == 1))
-        def _():
-            k = (turn - 2) // 2 + 4 * ((turn - 2) % 2)
+        @pl.when((turn >= 5) & (turn < 13) & (dist == 1))
+        def _():
+            k = (turn - 5) // 2 + 4 * ((turn - 5) % 2)
 
             @pl.when(feeds(k))
             def _():
@@ -493,20 +493,20 @@
     xv_copy = same(xv.at[c], partner, 3)
     s_slot(11)
     s_slot(12)
-    r_b.last()
     left1 = panel_of(1)
-    xv_copy.wait_recv()
-    inv0, inv1 = xv[0], xv[1]
     t10 = left1[0:BS].T
     mine = lt[...].reshape(512, BS).T
     ri = lax.broadcasted_iota(jnp.int32, (BS, 512), 0)
     ci = lax.broadcasted_iota(jnp.int32, (BS, 512), 1)
     unit = jnp.where(ci == ri + me * BS, -1.0, 0.0)
     a = jnp.where(me < 2, unit, mine)
+    xv_copy.wait_recv()
+    inv0, inv1 = xv[0], xv[1]
     w1 = mm(a[:, BS:], inv1)
     w0 = mm(a[:, :BS] - mm(w1, t10), inv0)
-
     wide = halves(jnp.concatenate([w0, w1], axis=1))
+    s_slot(13)
+    r_b.last()
 
     def left(d):
         cut = slice(d * BS, (d + 1) * BS)

time: 71.6 us -> 69.7 us (0.973)
  Pallas kernels: 68 us -> 66.2 us
    pallas_call x1, Pallas kernels: 68 us -> 66.2 us  [shards(): pl.pallas_call(kernel, out_shape=jax.ShapeDtypeStruct((BS * 8, 128), f32)...]
where the time goes in v6:
time: 69.7 us; the launch traced here: 68.9 us
  Pallas kernels  66.2 us (95%)
  local copies, waits for them, and re-layouts  2.65 us (4%)
    pallas_call x1, Pallas kernels, shards(): pl.pallas_call(kernel, out_shape=jax.ShapeDtypeStruct((BS * 8, 128), f32)...  66.2 us
    unnamed x5, local copies, waits for them, and re-layouts  2.65 us

profile of v6, /device:TPU:151, one launch (start us, length us, event | category | flops | bytes accessed | tf_op | source)
XLA Modules:
  0.0 68.9 jit_solution(17631422802783066515)
XLA Ops:
  0.0 0.0 copy-start
  0.0 0.8 %copy-done = f32[1,1,256,64]{2,3,1,0:T(8,128)S(1)} copy-done((f32[1,1,256,64]{2,3,1,0:T(8,128)S(1)}, f32[1,1,256,64]{2,3,1,0:T(8,128)}, u32[]{:S(2)}) %copy-start) | copy-done | bytes 65560
  0.8 0.0 copy-start.1
  0.8 0.8 %copy-done.1 = f32[4,1,256,16]{2,3,1,0:T(8,128)S(1)} copy-done((f32[4,1,256,16]{2,3,1,0:T(8,128)S(1)}, f32[4,1,256,16]{2,3,1,0:T(8,128)}, u32[]{:S(2)}) %copy-start.1) | copy-done | bytes 65560
  1.7 66.2 %shard_map.37 = f32[2048,128]{1,0:T(8,128)S(1)} custom-call(f32[256,8,128]{2,1,0:T(8,128)} %bitcast.11, f32[64,256]{1,0:T(8,128)S(1)} %bitcast.9, f32[4,16,256]{2,1,0:T(8,128)S(1)} %bitcast.10), custom_call_target="tpu_custom_call" | custom-call | tf_op jit(solution)/shard_map/pallas_call | solution.py:627
  67.9 1.0 %copy.6 = f32[1,1,256,4,1,256]{5,4,3,2,1,0:T(1,128)} copy(f32[1,1,256,4,1,256]{5,4,3,2,1,0:T(1,128)S(1)} %bitcast.8) | data formatting | bytes 2097152
Async XLA Ops:
  0.0 0.8 %copy-start = (f32[1,1,256,64]{2,3,1,0:T(8,128)S(1)}, f32[1,1,256,64]{2,3,1,0:T(8,128)}, u32[]{:S(2)}) copy-start(f32[1,1,256,64]{2,3,1,0:T(8,128)} %param.4) | copy-start | bytes 196612
  0.8 0.8 %copy-start.1 = (f32[4,1,256,16]{2,3,1,0:T(8,128)S(1)}, f32[4,1,256,16]{2,3,1,0:T(8,128)}, u32[]{:S(2)}) copy-start(f32[4,1,256,16]{2,3,1,0:T(8,128)} %param.5) | copy-start | bytes 196612

commit v7 on v6

--- a/solution.py
+++ b/solution.py
@@ -412,8 +412,8 @@
 
         return view
 
-    r_a = Across(blocks(0, R_CUT), 4, 3)
-    r_b = Along(blocks(R_CUT, 4 - R_CUT), 4, 3)
+    r_a = Across(blocks(0, R_CUT), 3, 4)
+    r_b = Along(blocks(R_CUT, 4 - R_CUT), 3, 4)
 
     class Panel:
         def __init__(self, ref):
@@ -581,15 +581,21 @@
         along[1].wait_recv()
         over[1].start()
 
+    def share(which, d):
+        rows = pl.ds(pl.multiple_of(which * BS, BS), BS)
+        return mm3(halves(yb[which]), (rh[d, rows], rl[d, rows]))
+
+    for d in range(4):
+        cut = slice(d * BS, (d + 1) * BS)
+        o_ref[:, cut] = o_ref[:, cut] - share(c, d)
+
     @pl.when((y != 0) | (c == 0))
     def _():
         for e in over:
             e.wait_recv()
 
-    both = halves(jnp.concatenate([yb[0], yb[1]], axis=1))
-
     def right(d):
-        return o_ref[:, d * BS : (d + 1) * BS] - mm3(both, (rh[d], rl[d]))
+        return o_ref[:, d * BS : (d + 1) * BS] - share(1 - c, d)
 
     for d in (1, 2, 3):
         write(d, right(d))

time: 69.7 us -> 68.9 us (0.989)
  no operation moved by 1% of the time
where the time goes in v7:
time: 68.9 us; the launch traced here: 68.7 us
  Pallas kernels  66 us (96%)
  local copies, waits for them, and re-layouts  2.65 us (4%)
    pallas_call x1, Pallas kernels, shards(): pl.pallas_call(kernel, out_shape=jax.ShapeDtypeStruct((BS * 8, 128), f32)...  66 us
    unnamed x5, local copies, waits for them, and re-layouts  2.65 us

profile of v7, /device:TPU:151, one launch (start us, length us, event | category | flops | bytes accessed | tf_op | source)
XLA Modules:
  0.0 68.7 jit_solution(8637799095657811559)
XLA Ops:
  0.0 0.0 copy-start
  0.0 0.8 %copy-done = f32[1,1,256,64]{2,3,1,0:T(8,128)S(1)} copy-done((f32[1,1,256,64]{2,3,1,0:T(8,128)S(1)}, f32[1,1,256,64]{2,3,1,0:T(8,128)}, u32[]{:S(2)}) %copy-start) | copy-done | bytes 65560
  0.8 0.0 copy-start.1
  0.8 0.8 %copy-done.1 = f32[4,1,256,16]{2,3,1,0:T(8,128)S(1)} copy-done((f32[4,1,256,16]{2,3,1,0:T(8,128)S(1)}, f32[4,1,256,16]{2,3,1,0:T(8,128)}, u32[]{:S(2)}) %copy-start.1) | copy-done | bytes 65560
  1.7 66.0 %shard_map.37 = f32[2048,128]{1,0:T(8,128)S(1)} custom-call(f32[256,8,128]{2,1,0:T(8,128)} %bitcast.11, f32[64,256]{1,0:T(8,128)S(1)} %bitcast.9, f32[4,16,256]{2,1,0:T(8,128)S(1)} %bitcast.10), custom_call_target="tpu_custom_call" | custom-call | tf_op jit(solution)/shard_map/pallas_call | solution.py:633
  67.7 1.0 %copy.6 = f32[1,1,256,4,1,256]{5,4,3,2,1,0:T(1,128)} copy(f32[1,1,256,4,1,256]{5,4,3,2,1,0:T(1,128)S(1)} %bitcast.8) | data formatting | bytes 2097152
Async XLA Ops:
  0.0 0.8 %copy-start = (f32[1,1,256,64]{2,3,1,0:T(8,128)S(1)}, f32[1,1,256,64]{2,3,1,0:T(8,128)}, u32[]{:S(2)}) copy-start(f32[1,1,256,64]{2,3,1,0:T(8,128)} %param.4) | copy-start | bytes 196612
  0.8 0.8 %copy-start.1 = (f32[4,1,256,16]{2,3,1,0:T(8,128)S(1)}, f32[4,1,256,16]{2,3,1,0:T(8,128)}, u32[]{:S(2)}) copy-start(f32[4,1,256,16]{2,3,1,0:T(8,128)} %param.5) | copy-start | bytes 196612

commit v8 on v7

--- a/solution.py
+++ b/solution.py
@@ -517,18 +517,19 @@
     left(0)
 
     def y_copy(half, dev, k, over):
-        part = yb.at[c, pl.ds(half * 128, 128)]
+        part = yb.at[c, pl.ds(half * 64, 64)]
         return pltpu.make_async_remote_copy(
             src_ref=part,
             dst_ref=part,
             send_sem=y_send.at[k],
-            recv_sem=y_recv.at[2 * over + half],
+            recv_sem=y_recv.at[4 * over + half],
             device_id=dev,
             device_id_type=MESH,
         )
 
-    over = [y_copy(h, partner, h, 1) for h in range(2)]
-    along = [y_copy(0, at_y(1), 2, 0), y_copy(1, at_y(-1), 3, 0), y_copy(1, at_y(1), 4, 0), y_copy(0, at_y(-1), 5, 0)]
+    over = [y_copy(q, partner, q, 1) for q in range(4)]
+    up = [y_copy(q, at_y(1), 4 + q, 0) for q in range(4)]
+    down = [y_copy(q, at_y(-1), 8 + q, 0) for q in range(4)]
 
     @pl.when(y == 0)
     def _():
@@ -541,8 +542,9 @@
         yb[c] = mm(o_ref[:, 0:BS], pair[1].T)
         for e in over:
             e.start()
-        for e in along:
-            e.start()
+        for q in range(4):
+            up[q].start()
+            down[(q + 2) % 4].start()
 
     for d in (1, 2, 3):
         left(d)
@@ -558,28 +560,24 @@
     t_sent()
     shares_sent()
 
+    def relay(order, onward):
+        for q in order:
+            up[q].wait_recv()
+            if q in onward:
+                onward[q].start()
+            over[q].start()
+
     @pl.when(y == 1)
     def _():
-        along[0].wait_recv()
-        along[0].start()
-        over[0].start()
-        along[1].wait_recv()
-        over[1].start()
+        relay((0, 1, 2, 3), {0: up[0], 1: up[1]})
 
     @pl.when(y == 3)
     def _():
-        along[1].wait_recv()
-        along[1].start()
-        over[1].start()
-        along[0].wait_recv()
-        over[0].start()
+        relay((2, 3, 0, 1), {2: down[2], 3: down[3]})
 
     @pl.when(y == 2)
     def _():
-        along[0].wait_recv()
-        over[0].start()
-        along[1].wait_recv()
-        over[1].start()
+        relay((0, 2, 1, 3), {})
 
     def share(which, d):
         rows = pl.ds(pl.multiple_of(which * BS, BS), BS)
@@ -613,16 +611,18 @@
 
     @pl.when((y == 0) | (y == 1))
     def _():
-        along[0].wait_send()
+        up[0].wait_send()
+        up[1].wait_send()
 
     @pl.when((y == 0) | (y == 3))
     def _():
-        along[1].wait_send()
+        down[2].wait_send()
+        down[3].wait_send()
 
     @pl.when(y == 0)
     def _():
-        along[2].wait_send()
-        along[3].wait_send()
+        for e in (up[2], up[3], down[0], down[1]):
+            e.wait_send()
 
 
 N_EVENTS = 70
@@ -658,8 +658,8 @@
             pltpu.SemaphoreType.DMA((3, 8)),
             pltpu.SemaphoreType.DMA((5,)),
             pltpu.SemaphoreType.DMA((13,)),
-            pltpu.SemaphoreType.DMA((6,)),
-            pltpu.SemaphoreType.DMA((4,)),
+            pltpu.SemaphoreType.DMA((12,)),
+            pltpu.SemaphoreType.DMA((8,)),
         ],
         compiler_params=pltpu.CompilerParams(collective_id=0, has_side_effects=True, vmem_limit_bytes=55000000),
     )(

time: 68.9 us -> 68.3 us (level)
  no operation moved by 1% of the time
where the time goes in v8:
time: 68.3 us; the launch traced here: 68.1 us
  Pallas kernels  65.4 us (96%)
  local copies, waits for them, and re-layouts  2.65 us (4%)
    pallas_call x1, Pallas kernels, shards(): pl.pallas_call(kernel, out_shape=jax.ShapeDtypeStruct((BS * 8, 128), f32)...  65.4 us
    unnamed x5, local copies, waits for them, and re-layouts  2.65 us

profile of v8, /device:TPU:151, one launch (start us, length us, event | category | flops | bytes accessed | tf_op | source)
XLA Modules:
  0.0 68.1 jit_solution(7455733358125488850)
XLA Ops:
  0.0 0.0 copy-start
  0.0 0.8 %copy-done = f32[1,1,256,64]{2,3,1,0:T(8,128)S(1)} copy-done((f32[1,1,256,64]{2,3,1,0:T(8,128)S(1)}, f32[1,1,256,64]{2,3,1,0:T(8,128)}, u32[]{:S(2)}) %copy-start) | copy-done | bytes 65560
  0.8 0.0 copy-start.1
  0.8 0.8 %copy-done.1 = f32[4,1,256,16]{2,3,1,0:T(8,128)S(1)} copy-done((f32[4,1,256,16]{2,3,1,0:T(8,128)S(1)}, f32[4,1,256,16]{2,3,1,0:T(8,128)}, u32[]{:S(2)}) %copy-start.1) | copy-done | bytes 65560
  1.7 65.4 %shard_map.37 = f32[2048,128]{1,0:T(8,128)S(1)} custom-call(f32[256,8,128]{2,1,0:T(8,128)} %bitcast.11, f32[64,256]{1,0:T(8,128)S(1)} %bitcast.9, f32[4,16,256]{2,1,0:T(8,128)S(1)} %bitcast.10), custom_call_target="tpu_custom_call" | custom-call | tf_op jit(solution)/shard_map/pallas_call | solution.py:633
  67.1 1.0 %copy.6 = f32[1,1,256,4,1,256]{5,4,3,2,1,0:T(1,128)} copy(f32[1,1,256,4,1,256]{5,4,3,2,1,0:T(1,128)S(1)} %bitcast.8) | data formatting | bytes 2097152
Async XLA Ops:
  0.0 0.8 %copy-start = (f32[1,1,256,64]{2,3,1,0:T(8,128)S(1)}, f32[1,1,256,64]{2,3,1,0:T(8,128)}, u32[]{:S(2)}) copy-start(f32[1,1,256,64]{2,3,1,0:T(8,128)} %param.4) | copy-start | bytes 196612
  0.8 0.8 %copy-start.1 = (f32[4,1,256,16]{2,3,1,0:T(8,128)S(1)}, f32[4,1,256,16]{2,3,1,0:T(8,128)}, u32[]{:S(2)}) copy-start(f32[4,1,256,16]{2,3,1,0:T(8,128)} %param.5) | copy-start | bytes 196612

commit v9 on v8

--- a/solution.py
+++ b/solution.py
@@ -12,7 +12,7 @@
 NZ = 8
 NY = 4
 R_CUT = 2
-LAG = 2
+LAG = 3
 MESH = pl.DeviceIdType.MESH
 
 

time: 68.3 us -> 68.6 us (level)
  no operation moved by 1% of the time
where the time goes in v9:
time: 68.6 us; the launch traced here: 68.4 us
  Pallas kernels  65.7 us (96%)
  local copies, waits for them, and re-layouts  2.65 us (4%)
    pallas_call x1, Pallas kernels, shards(): pl.pallas_call(kernel, out_shape=jax.ShapeDtypeStruct((BS * 8, 128), f32)...  65.7 us
    unnamed x5, local copies, waits for them, and re-layouts  2.65 us

profile of v9, /device:TPU:151, one launch (start us, length us, event | category | flops | bytes accessed | tf_op | source)
XLA Modules:
  0.0 68.4 jit_solution(1090445745888387408)
XLA Ops:
  0.0 0.0 copy-start
  0.0 0.8 %copy-done = f32[1,1,256,64]{2,3,1,0:T(8,128)S(1)} copy-done((f32[1,1,256,64]{2,3,1,0:T(8,128)S(1)}, f32[1,1,256,64]{2,3,1,0:T(8,128)}, u32[]{:S(2)}) %copy-start) | copy-done | bytes 65560
  0.8 0.0 copy-start.1
  0.8 0.8 %copy-done.1 = f32[4,1,256,16]{2,3,1,0:T(8,128)S(1)} copy-done((f32[4,1,256,16]{2,3,1,0:T(8,128)S(1)}, f32[4,1,256,16]{2,3,1,0:T(8,128)}, u32[]{:S(2)}) %copy-start.1) | copy-done | bytes 65560
  1.7 65.7 %shard_map.37 = f32[2048,128]{1,0:T(8,128)S(1)} custom-call(f32[256,8,128]{2,1,0:T(8,128)} %bitcast.11, f32[64,256]{1,0:T(8,128)S(1)} %bitcast.9, f32[4,16,256]{2,1,0:T(8,128)S(1)} %bitcast.10), custom_call_target="tpu_custom_call" | custom-call | tf_op jit(solution)/shard_map/pallas_call | solution.py:633
  67.4 1.0 %copy.6 = f32[1,1,256,4,1,256]{5,4,3,2,1,0:T(1,128)} copy(f32[1,1,256,4,1,256]{5,4,3,2,1,0:T(1,128)S(1)} %bitcast.8) | data formatting | bytes 2097152
Async XLA Ops:
  0.0 0.8 %copy-start = (f32[1,1,256,64]{2,3,1,0:T(8,128)S(1)}, f32[1,1,256,64]{2,3,1,0:T(8,128)}, u32[]{:S(2)}) copy-start(f32[1,1,256,64]{2,3,1,0:T(8,128)} %param.4) | copy-start | bytes 196612
  0.8 0.8 %copy-start.1 = (f32[4,1,256,16]{2,3,1,0:T(8,128)S(1)}, f32[4,1,256,16]{2,3,1,0:T(8,128)}, u32[]{:S(2)}) copy-start(f32[4,1,256,16]{2,3,1,0:T(8,128)} %param.5) | copy-start | bytes 196612
